TPU v7x, 256 devices: a whole 4x4x8 slice. The times are simulated.
256 devices in a mesh: seq: 64 (over y, z, core), layer: 4 (over x).
Axes of the slice: x: 4, y: 4, z: 8, core: 2. Of those that a mesh axis runs over, the one named last changes fastest.
Arguments:
- gradients: bfloat16 [16384, 4096], P('seq', 'layer'), may hold values from -6 to 6
- projection: bfloat16 [4096, 8192], P('layer', 'seq'), may hold values from -0.09375 to 0.09375
- queries: bfloat16 [256, 8192], P(None, 'seq'), may hold values from -6 to 6
Outputs:
- scores: float32 [16384, 256], P(('seq', 'layer'))
All inputs are finite; a program needn't handle non-finite values.
Results may differ from a plain program's by a relative error of at most 0.0029.
Values may be sent and summed in bfloat16 or wider, within the bound.
A program may use at most 128 MiB of HBM per device.

v0:
```python
import math

import jax
import jax.numpy as jnp
from jax import lax
from jax.sharding import PartitionSpec as P

K = 8192


epsilon = 1e-06


def copy_for_each(array, axis):
    size = lax.axis_size(axis)
    return lax.all_to_all(
        jnp.broadcast_to(array[None], (size, *array.shape)), axis, 0, 0, tiled=True
    )


def joined_along(parts, dim):
    lengths = list(parts.shape[1:])
    lengths[dim] *= parts.shape[0]
    return jnp.moveaxis(parts, 0, dim).reshape(lengths)


def collect(array, axis, dim):
    parts = copy_for_each(array, axis)
    return joined_along(parts, dim)


def split_up(array, dim, size):
    before, after = (array.shape[:dim], array.shape[dim + 1 :])
    return jnp.moveaxis(array.reshape(*before, size, -1, *after), dim, 0)


def summed_on_arrival(array, axis, dim):
    parts = split_up(array, dim, lax.axis_size(axis))
    arrived = lax.all_to_all(parts, axis, split_axis=0, concat_axis=0, tiled=True)
    return arrived.sum(axis=0)


def side_by_side(arrays, axis, dim, along):
    widths = [math.prod(a.shape[along:]) for a in arrays]
    both = jnp.concatenate(
        [a.reshape(*a.shape[:along], w) for a, w in zip(arrays, widths)], axis=along
    )
    out = summed_on_arrival(both, axis, dim)
    parts = jnp.split(out, [sum(widths[:k]) for k in range(1, len(widths))], axis=along)
    return tuple((b.reshape(*out.shape[:along], *a.shape[along:]) for a, b in zip(arrays, parts)))


def of_everyone(array, axis):
    return copy_for_each(array, axis).sum(axis=0)


def scaled(products, row_squares, query_squares):
    return (
        math.sqrt(K)
        * products
        * lax.rsqrt(row_squares + epsilon)[:, None]
        * lax.rsqrt(query_squares + epsilon)[None, :]
    )


def finish_blocks(gradients, projection, queries, layers):
    full_grads = collect(gradients, "layer", 1)
    columns = projection.shape[1] // layers
    block = lax.all_to_all(projection, "layer", split_axis=1, concat_axis=0, tiled=True)
    sketch = jnp.dot(
        full_grads,
        lax.all_gather(block, "seq", axis=1, tiled=True),
        preferred_element_type=jnp.float32,
    ).astype(jnp.bfloat16)
    position = lax.axis_index("layer")
    own_queries = lax.dynamic_slice_in_dim(queries, position * columns, columns, 1)
    query_part = collect(own_queries, "seq", 1)
    sketch_wide = sketch.astype(jnp.float32)
    row_partial = jnp.sum(sketch_wide * sketch_wide, axis=1)
    query_wide = query_part.astype(jnp.float32)
    query_partial = jnp.sum(query_wide * query_wide, axis=1)
    partial_products = lax.dot_general(
        sketch, query_part, (((1,), (1,)), ((), ())), preferred_element_type=jnp.float32
    )
    products, row_squares = side_by_side((partial_products, row_partial), "layer", 0, 1)
    query_squares = of_everyone(query_partial, "layer")
    return scaled(products, row_squares, query_squares)


def shards(gradients, projection, queries):
    layers = lax.axis_size("layer")
    return finish_blocks(gradients, projection, queries, layers)


def solution(mesh):
    placed = (P("seq", "layer"), P("layer", "seq"), P(None, "seq"))
    return jax.shard_map(
        shards, mesh=mesh, in_specs=placed, out_specs=P(("seq", "layer"), None), check_vma=False
    )
```

profile of v0, /device:TPU:1, one launch (start us, length us, event | category | flops | bytes accessed | tf_op | source)
XLA Modules:
  0.0 160.2 jit_solution(9524027480819616541)
XLA Ops:
  6.5 0.0 copy-start
  6.5 0.0 all-gather.2.cloned.1.call-start
  6.5 1.1 copy.17
  7.7 10.2 %all_to_all.40 = bf16[1024,4,32]{0,2,1:T(8,128)(2,1)S(1)} all-to-all(bf16[1024,4,32]{0,2,1:T(8,128)(2,1)S(1)} %bitcast.23), channel_id=1, replica_groups=mesh['seq'=64,'layer'=4] {'layer'}, dimensions={1} | all-to-all | bytes 524288 | tf_op jit(solution)/shard_map/all_to_all | solution.py:69
  17.9 0.7 copy.26
  18.6 0.0 all-gather.2.cloned.1.call-update
  18.6 0.0 copy-done
  18.6 0.1 constant_dynamic-slice_fusion
  18.7 0.1 copy.19
  18.8 0.0 copy-start.1
  18.8 0.1 broadcast_in_dim.7
  18.9 51.0 %all_to_all.41 = bf16[64,256,32]{1,2,0:T(8,128)(2,1)S(1)} all-to-all(bf16[64,256,32]{1,2,0:T(8,128)(2,1)S(1)} %broadcast_in_dim.7), channel_id=1, replica_groups=mesh['seq'=64,'layer'=4] {'seq'}, dimensions={0} | all-to-all | bytes 2097152 | tf_op jit(solution)/shard_map/all_to_all | solution.py:16
  70.0 0.3 multiply_reduce_fusion
  70.3 0.6 broadcast_in_dim.8
  70.9 3.2 %all-to-all-start.4 = ((f32[4,1,256]{2,1,0:T(1,128)}), f32[4,1,256]{2,1,0:T(1,128)S(1)}, u32[]{:S(2)}, u32[]{:S(2)}) async-start(f32[4,1,256]{2,1,0:T(1,128)} %broadcast_in_dim.8), calls=%async_computation.4 | async-start | bytes 8192 | tf_op jit(solution)/shard_map/all_to_all | solution.py:16
  74.1 0.0 copy-done.1
  74.1 0.2 copy.16
  74.3 3.9 %all-to-all-done.4 = f32[4,1,256]{2,1,0:T(1,128)S(1)} async-done(((f32[4,1,256]{2,1,0:T(1,128)}), f32[4,1,256]{2,1,0:T(1,128)S(1)}, u32[]{:S(2)}, u32[]{:S(2)}) %all-to-all-start.4) | async-done | bytes 4128 | tf_op jit(solution)/shard_map/all_to_all | solution.py:16
  78.2 1.5 broadcast_in_dim.6
  79.7 3.6 %all-to-all-start = ((bf16[4,256,1024]{1,2,0:T(8,128)(2,1)}), bf16[4,256,1024]{1,2,0:T(8,128)(2,1)S(1)}, u32[]{:S(2)}, u32[]{:S(2)}) async-start(bf16[4,256,1024]{1,2,0:T(8,128)(2,1)} %broadcast_in_dim.6), calls=%async_computation | async-start | bytes 4194304 | tf_op jit(solution)/shard_map/all_to_all | solution.py:16
  83.4 26.0 %all-to-all-done = bf16[4,256,1024]{1,2,0:T(8,128)(2,1)S(1)} async-done(((bf16[4,256,1024]{1,2,0:T(8,128)(2,1)}), bf16[4,256,1024]{1,2,0:T(8,128)(2,1)S(1)}, u32[]{:S(2)}, u32[]{:S(2)}) %all-to-all-start) | async-done | bytes 2097184 | tf_op jit(solution)/shard_map/all_to_all | solution.py:16
  109.4 19.4 %all-gather.2.cloned.1.call-done = bf16[4096,2048]{0,1:T(8,128)(2,1)} async-done(((bf16[4096,32]{0,1:T(8,128)(2,1)}), bf16[4096,2048]{0,1:T(8,128)(2,1)}) %all-gather.2.cloned.1.call-update) | async-done | bytes 16777232 | tf_op jit(solution)/shard_map/all_gather | solution.py:72
  128.8 9.4 %multiply_reduce_fusion.1 = (f32[256]{0:T(256)S(1)}, bf16[256,2048]{1,0:T(8,128)(2,1)}) fusion(bf16[256,4096]{0,1:T(8,128)(2,1)S(1)} %bitcast.19, bf16[4096,2048]{0,1:T(8,128)(2,1)} %all-gather.2.cloned.1.call-done), kind=kOutput, calls=%fused_computation.2 | convolution fusion | flops 4297064448 | bytes 19923968 | tf_op jit(solution)/shard_map/dot_general | solution.py:70
  138.2 0.2 concatenate.8
  138.4 1.7 %fusion.4 = f32[4,64,256]{2,1,0:T(8,128)S(1)} fusion(bf16[4,64,2048]{2,1,0:T(8,128)(2,1)} %bitcast.20, bf16[256,2048,1]{0,1,2:T(8,128)(2,1)S(1)} %bitcast.18), kind=kOutput, calls=%fused_computation.12 | convolution fusion | flops 268435456 | bytes 2359296 | tf_op jit(solution)/shard_map/dot_general | solution.py:82
  140.1 0.8 pad_maximum_fusion
  140.9 4.0 %all-to-all-start.3 = ((f32[4,64,257]{2,1,0:T(8,128)}), f32[4,64,257]{2,1,0:T(8,128)S(1)}, u32[]{:S(2)}, u32[]{:S(2)}) async-start(f32[4,64,257]{2,1,0:T(8,128)} %pad_maximum_fusion), calls=%async_computation.3 | async-start | bytes 786432 | tf_op jit(solution)/shard_map/all_to_all | solution.py:39
  144.8 7.6 %all-to-all-done.3 = f32[4,64,257]{2,1,0:T(8,128)S(1)} async-done(((f32[4,64,257]{2,1,0:T(8,128)}), f32[4,64,257]{2,1,0:T(8,128)S(1)}, u32[]{:S(2)}, u32[]{:S(2)}) %all-to-all-start.3) | async-done | bytes 263200 | tf_op jit(solution)/shard_map/all_to_all | solution.py:39
  152.5 0.1 fusion.3
  152.6 0.7 fusion
  (3 shorter events, 0.1 us)
Async XLA Ops:
  6.5 12.1 %copy-start = (bf16[256,128]{1,0:T(8,128)(2,1)S(1)}, bf16[256,128]{1,0:T(8,128)(2,1)}, u32[]{:S(2)}) copy-start(bf16[256,128]{1,0:T(8,128)(2,1)} %param.5) | copy-start | bytes 196612
  6.5 122.2 %all-gather.2.cloned.1.call-start = ((), (), s32[]{:S(2)}) async-start(), calls=%async_computation.5 | async-start | bytes 17039360 | tf_op jit(solution)/shard_map/all_gather | solution.py:72
  18.8 55.3 %copy-start.1 = (bf16[256,1024]{1,0:T(8,128)(2,1)S(1)}, bf16[256,1024]{1,0:T(8,128)(2,1)}, u32[]{:S(2)}) copy-start(bf16[256,1024]{1,0:T(8,128)(2,1)} %param.3) | copy-start | bytes 1572868
  70.9 7.4 %all-to-all-start.4 = ((f32[4,1,256]{2,1,0:T(1,128)}), f32[4,1,256]{2,1,0:T(1,128)S(1)}, u32[]{:S(2)}, u32[]{:S(2)}) async-start(f32[4,1,256]{2,1,0:T(1,128)} %broadcast_in_dim.8), calls=%async_computation.4 | async-start | bytes 8192 | tf_op jit(solution)/shard_map/all_to_all | solution.py:16
  79.7 29.7 %all-to-all-start = ((bf16[4,256,1024]{1,2,0:T(8,128)(2,1)}), bf16[4,256,1024]{1,2,0:T(8,128)(2,1)S(1)}, u32[]{:S(2)}, u32[]{:S(2)}) async-start(bf16[4,256,1024]{1,2,0:T(8,128)(2,1)} %broadcast_in_dim.6), calls=%async_computation | async-start | bytes 4194304 | tf_op jit(solution)/shard_map/all_to_all | solution.py:16
  140.9 11.6 %all-to-all-start.3 = ((f32[4,64,257]{2,1,0:T(8,128)}), f32[4,64,257]{2,1,0:T(8,128)S(1)}, u32[]{:S(2)}, u32[]{:S(2)}) async-start(f32[4,64,257]{2,1,0:T(8,128)} %pad_maximum_fusion), calls=%async_computation.3 | async-start | bytes 786432 | tf_op jit(solution)/shard_map/all_to_all | solution.py:39
Sparse Core Ops, SparseCore 0:
  18.7 109.9 all-gather.1
where the time goes:
time: 161 us; the launch traced here: 160 us
  blocking collectives  61.2 us (38%)
  waiting for transfers between devices  56.9 us (35%)
  between operations  13.5 us (8%)
  matrix products  11.1 us (7%)
  starting transfers between devices  10.8 us (7%)
  local copies, waits for them, and re-layouts  4.64 us (3%)
  other arithmetic  1.97 us (1%)
    all_to_all x1, blocking collectives, copy_for_each(): lax.all_to_all(jnp.broadcast_to(array[None], (size, *array.shape)), axis,...  51 us
    all_to_all x2, waiting for transfers between devices, copy_for_each(): lax.all_to_all(jnp.broadcast_to(array[None], (size, *array.shape)), axis,...  29.9 us
    all_gather x1, waiting for transfers between devices, finish_blocks(): lax.all_gather(block, 'seq', axis=1, tiled=True)  19.4 us
    all_to_all x1, blocking collectives, finish_blocks(): lax.all_to_all(projection, 'layer', split_axis=1, concat_axis=0, tiled=True)  10.2 us
    dot_general x1, matrix products, finish_blocks(): jnp.dot(full_grads, lax.all_gather(block, 'seq', axis=1, tiled=True), pre...  9.43 us
    all_to_all x1, waiting for transfers between devices, summed_on_arrival(): lax.all_to_all(parts, axis, split_axis=0, concat_axis=0, tiled=True)  7.62 us
    all_to_all x2, starting transfers between devices, copy_for_each(): lax.all_to_all(jnp.broadcast_to(array[None], (size, *array.shape)), axis,...  6.85 us
    all_to_all x1, starting transfers between devices, summed_on_arrival(): lax.all_to_all(parts, axis, split_axis=0, concat_axis=0, tiled=True)  3.96 us
  transfers between devices with their start and end apart: 4, of which 4 were waited for; matrix products, arithmetic and copies ran while one was open for 2% of the time, Pallas kernels for 0%

commit v1 on v0

v1 whole, which is shorter than its diff:
```python
import functools
import heapq
import math

import jax
import jax.numpy as jnp
from jax import lax
from jax.experimental import pallas as pl
from jax.experimental.pallas import tpu as pltpu
from jax.sharding import PartitionSpec as P

MESH = pl.DeviceIdType.MESH
K = 8192
EPS = 1e-06
YS, ZS, XS = 4, 8, 4
ROWS_A = 448


def halves(first, last):
    mid = (first + last) // 2
    return {0: (first, last), 1: (first, mid), 2: (mid, last)}


def step(pos, by, size):
    return (pos + by) % size


def forwards(key):
    part, oy, oz, half = key
    out = []
    zs = [("z+", (part, oy, 7, 0)), ("z-", (part, oy, 1, 0))]
    ys = [("y+", (part, 3, oz, 0)), ("y-", (part, 1, oz, 0))]
    on_y = {3: [("y+", (part, 2, oz, 1))], 1: [("y-", (part, 2, oz, 2))]}
    on_z = {
        7: [("z+", (part, oy, 6, 0))],
        6: [("z+", (part, oy, 5, 0))],
        5: [("z+", (part, oy, 4, 1))],
        1: [("z-", (part, oy, 2, 0))],
        2: [("z-", (part, oy, 3, 0))],
        3: [("z-", (part, oy, 4, 2))],
    }
    if part == "A":
        if oz == 0:
            out += ys if oy == 0 else on_y.get(oy, [])
            out += zs
        else:
            out += on_z.get(oz, [])
    else:
        if oy == 0:
            out += zs if oz == 0 else on_z.get(oz, [])
            out += ys
        else:
            out += on_y.get(oy, [])
    return out


def plan(bytes_a, bytes_b):
    rate, lag, quad_us, gather_us = 44e3, 1.8, 0.45, 20.0
    free = dict.fromkeys(["y+", "y-", "z+", "z-"], 0.0)
    size = {"A": bytes_a, "B": bytes_b}
    arrivals, order, actions = [], 0, []
    seen, whole, mine, theirs = set(), set(), {}, {}
    quads = []
    now = 0.0

    def complete(key):
        nonlocal order
        part, oy, oz, half = key
        sent = []
        for link, new in forwards(key):
            start = max(now, free[link])
            free[link] = start + size[part] / (2 if new[3] else 1) / rate
            heapq.heappush(arrivals, (free[link] + lag, order, new))
            order += 1
            sent.append((link, new))
        actions.append(("send", key[:3], sent))
        seen.add(key[:3])
        if ("A", oy, oz) in seen and ("B", oy, oz) in seen:
            actions.append(("share", oy, oz))
            mine[oz] = mine.get(oz, 0) + 1
            if mine[oz] == YS:
                quads.append((now, oz, 0))
                quads.append((now + 2.0, oz, 1))

    complete(("A", 0, 0, 0))
    complete(("B", 0, 0, 0))
    got = {}
    gathered = False
    while arrivals or quads or not gathered:
        if not gathered and now >= gather_us:
            actions.append(("gradients",))
            gathered = True
        if arrivals and arrivals[0][0] <= now:
            _, _, key = heapq.heappop(arrivals)
            actions.append(("wait", key))
            now += 0.08
            part, oy, oz, half = key
            if half:
                got[key[:3]] = got.get(key[:3], 0) + 1
                if got[key[:3]] == 2:
                    complete(key)
            else:
                complete(key)
            continue
        ready = sorted(q for q in quads if q[0] <= now)
        if gathered and ready:
            quads.remove(ready[0])
            actions.append(("quad", ready[0][1], ready[0][2]))
            now += quad_us
            continue
        nexts = [a[0] for a in arrivals[:1]] + ([min(quads)[0]] if quads and gathered else [])
        if not gathered:
            nexts.append(gather_us)
        now = max(now + 1e-6, min(nexts))
    return actions, now


def kernel(actions, spans, ids, g_hbm, p_hbm, q_hbm, out_ref, gall, pin, qin, buf, acc, fsend, frecv,
           local, gs, gr, ts, tr, ms, mr, ds, dr, fs, fr):
    s, a = lax.axis_index("seq"), lax.axis_index("layer")
    core, z, y = s % 2, (s // 2) % ZS, s // (2 * ZS)
    feats, width = p_hbm.shape
    part_rows = q_hbm.shape[0] // XS
    mine = 2 * (z % 2) + core
    swap_s = s - mine + a
    partner = s + 1 - 2 * core

    def at(yy, zz):
        return (yy * ZS + zz) * 2 + core

    ahead = {
        "y+": (at((y + 1) % YS, z), a),
        "y-": (at((y + YS - 1) % YS, z), a),
        "z+": (at(y, (z + 1) % ZS), a),
        "z-": (at(y, (z + ZS - 1) % ZS), a),
        "x+": (s, (a + 1) % XS),
        "x-": (s, (a + XS - 1) % XS),
        "x2": (s, (a + 2) % XS),
    }
    ypos = [(y + k) % YS for k in range(YS)]
    zpos = [(z + k) % ZS for k in range(ZS)]

    def remote(src, dst, send, recv, to):
        return pltpu.make_async_remote_copy(
            src_ref=src, dst_ref=dst, send_sem=send, recv_sem=recv, device_id=to, device_id_type=MESH
        )

    p_in = pltpu.make_async_copy(p_hbm, pin, local.at[0])
    q_in = pltpu.make_async_copy(q_hbm, qin, local.at[1])
    g_in = pltpu.make_async_copy(g_hbm, gall.at[a], local.at[2])
    p_in.start()
    q_in.start()
    g_in.start()

    barrier = pltpu.get_barrier_semaphore()
    around = [*ahead.values(), (partner, a)]
    for device in around:
        pl.semaphore_signal(barrier, inc=1, device_id=device, device_id_type=MESH)

    @pl.when(a != mine)
    def _():
        pl.semaphore_signal(barrier, inc=1, device_id=(swap_s, mine), device_id_type=MESH)

    @pl.when(a != mine)
    def _():
        pl.semaphore_wait(barrier, len(around) + 1)

    @pl.when(a == mine)
    def _():
        pl.semaphore_wait(barrier, len(around))

    q_rows = qin.at[pl.ds(pl.multiple_of(a * part_rows, part_rows), part_rows)]
    p_swap = remote(pin, buf.at[swap_s, pl.ds(0, feats)], ts.at[0], tr.at[0], (swap_s, mine))
    q_swap = remote(q_rows, buf.at[swap_s, pl.ds(feats, part_rows)], ts.at[1], tr.at[1], (swap_s, mine))
    p_stay = pltpu.make_async_copy(pin, buf.at[s, pl.ds(0, feats)], local.at[3])
    q_stay = pltpu.make_async_copy(q_rows, buf.at[s, pl.ds(feats, part_rows)], local.at[4])
    p_in.wait()
    q_in.wait()

    @pl.when(a != mine)
    def _():
        p_swap.start()
        q_swap.start()

    @pl.when(a == mine)
    def _():
        p_stay.start()
        q_stay.start()

    left, right, far = (a + XS - 1) % XS, (a + 1) % XS, (a + 2) % XS
    half = gall.shape[1] // 2
    g_sends = [
        remote(gall.at[a], gall.at[a], gs.at[0], gr.at[0], ahead["x+"]),
        remote(gall.at[a], gall.at[a], gs.at[1], gr.at[1], ahead["x-"]),
        remote(gall.at[left, pl.ds(0, half)], gall.at[left, pl.ds(0, half)], gs.at[2], gr.at[2], ahead["x+"]),
        remote(gall.at[right, pl.ds(half, half)], gall.at[right, pl.ds(half, half)], gs.at[3], gr.at[3], ahead["x-"]),
    ]
    g_waits = [
        remote(gall.at[left], gall.at[left], gs.at[0], gr.at[0], ahead["x+"]),
        remote(gall.at[right], gall.at[right], gs.at[1], gr.at[1], ahead["x-"]),
        remote(gall.at[far, pl.ds(0, half)], gall.at[far, pl.ds(0, half)], gs.at[2], gr.at[2], ahead["x+"]),
        remote(gall.at[far, pl.ds(half, half)], gall.at[far, pl.ds(half, half)], gs.at[3], gr.at[3], ahead["x-"]),
    ]
    g_in.wait()
    g_sends[0].start()
    g_sends[1].start()

    @pl.when(a != mine)
    def _():
        remote(pin, buf.at[s, pl.ds(0, feats)], ts.at[0], tr.at[0], (swap_s, mine)).wait_recv()
        remote(q_rows, buf.at[s, pl.ds(feats, part_rows)], ts.at[1], tr.at[1], (swap_s, mine)).wait_recv()

    @pl.when(a == mine)
    def _():
        p_stay.wait()
        q_stay.wait()

    def block(key):
        part, oy, oz, which = key
        first, last = spans[part][which]
        return buf.at[at(ypos[oy], zpos[oz]), pl.ds(first, last - first)]

    def message(link, key, view):
        return remote(view, view, ms.at[ids[key]], mr.at[ids[key]], ahead[link])

    def shared(oy, oz, whose):
        view = buf.at[whose + ((ypos[oy] * ZS + zpos[oz]) * 2)]
        return remote(view, view, ds.at[oy * ZS + oz], dr.at[oy * ZS + oz], (partner, a))

    for oz in range(acc.shape[0]):
        acc[oz] = jnp.zeros(acc.shape[1:], jnp.float32)

    def quad(zz, whose):
        layer = 2 * (zz % 2) + whose
        for pair in range(2):
            right_side = jnp.concatenate(
                [buf[(yy * ZS + zz) * 2 + whose, pl.ds(0, feats), :] for yy in (2 * pair, 2 * pair + 1)], axis=1
            )
            columns = pl.ds(pair * 2 * width, 2 * width)
            acc[zz // 2, :, columns] += jnp.dot(gall[layer], right_side, preferred_element_type=jnp.float32)

    used = {}
    for action in actions:
        if action[0] == "send":
            for link, new in action[2]:
                source = (*action[1], new[3])
                used[new] = link
                message(link, new, block(source)).start()
        elif action[0] == "share":
            shared(action[1], action[2], core).start()
        elif action[0] == "wait":
            key = action[1]
            message(used[key], key, block(key)).wait_recv()
        elif action[0] == "gradients":
            g_waits[0].wait_recv()
            g_sends[2].start()
            g_waits[1].wait_recv()
            g_sends[3].start()
            g_waits[2].wait_recv()
            g_waits[3].wait_recv()
        elif action[0] == "quad":
            oz, other = action[1:]
            if other:
                for oy in range(YS):
                    shared(oy, oz, 1 - core).wait_recv()
                quad(zpos[oz], 1 - core)
            else:
                quad(zpos[oz], core)

    rows = gall.shape[1]
    queries = q_hbm.shape[0]
    products = jnp.zeros((rows, queries), jnp.float32)
    row_squares = jnp.zeros((rows, width), jnp.float32)
    query_squares = jnp.zeros((queries, width), jnp.float32)

    def finish(group, carry):
        products, row_squares, query_squares = carry
        sketch = acc[group].astype(jnp.bfloat16)
        wide = sketch.astype(jnp.float32)
        asked = jnp.concatenate(
            [
                jnp.concatenate(
                    [buf[yy * 2 * ZS + group * 4 + layer, pl.ds(feats, part_rows), :] for layer in range(XS)], axis=0
                )
                for yy in range(YS)
            ],
            axis=1,
        )
        asked_wide = asked.astype(jnp.float32)
        for yy in range(YS):
            own = wide[:, yy * width : (yy + 1) * width]
            row_squares += own * own
            ask = asked_wide[:, yy * width : (yy + 1) * width]
            query_squares += ask * ask
        products += lax.dot_general(
            sketch, asked, (((1,), (1,)), ((), ())), preferred_element_type=jnp.float32
        )
        return products, row_squares, query_squares

    products, row_squares, query_squares = lax.fori_loop(
        0, acc.shape[0], finish, (products, row_squares, query_squares)
    )
    ones = jnp.ones((8, width), jnp.float32)

    def along(squares):
        return lax.dot_general(
            ones, squares, (((1,), (1,)), ((), ())), precision=lax.Precision.HIGHEST,
            preferred_element_type=jnp.float32,
        )

    block_rows = rows // XS
    row_line, query_line = along(row_squares), along(query_squares)
    for target in range(XS):
        fsend[target, pl.ds(0, block_rows)] = products[target * block_rows : (target + 1) * block_rows]
        fsend[target, pl.ds(block_rows, 8)] = row_line
        fsend[target, pl.ds(block_rows + 8, 8)] = query_line
    finals = []
    for k, link in ((1, "x+"), (3, "x-"), (2, "x2")):
        target = (a + k) % XS
        finals.append(remote(fsend.at[target], frecv.at[k - 1], fs.at[k - 1], fr.at[k - 1], ahead[link]))
    for copy in finals:
        copy.start()
    total = fsend[a]
    for copy in finals:
        copy.wait_recv()
    total = total + frecv[0] + frecv[1] + frecv[2]
    at_row = lax.broadcasted_iota(jnp.int32, (block_rows, rows), 0) + a * block_rows
    chosen = (lax.broadcasted_iota(jnp.int32, (block_rows, rows), 1) == at_row).astype(jnp.float32)
    own_rows = lax.dot_general(
        chosen, total[block_rows : block_rows + 8], (((1,), (1,)), ((), ())), precision=lax.Precision.HIGHEST,
        preferred_element_type=jnp.float32,
    )[:, 0:1]
    asked_squares = total[block_rows + 8 : block_rows + 9]
    out_ref[...] = (
        math.sqrt(K) * total[:block_rows] * lax.rsqrt(own_rows + EPS) * lax.rsqrt(asked_squares + EPS)
    )

    for copy in finals:
        copy.wait_send()
    for copy in g_sends:
        copy.wait_send()

    @pl.when(a != mine)
    def _():
        p_swap.wait_send()
        q_swap.wait_send()

    groups = {}
    for key in ids:
        groups.setdefault((key[0], bool(key[3])), []).append(key)
    for keys in groups.values():
        first, view = ids[keys[0]], block(keys[0])

        def sent(k, carry, view=view):
            remote(view, view, ms.at[k], mr.at[k], (partner, a)).wait_send()
            return carry

        lax.fori_loop(first, first + len(keys), sent, 0)

    def given(k, carry):
        remote(buf.at[s], buf.at[s], ds.at[k], dr.at[k], (partner, a)).wait_send()
        return carry

    lax.fori_loop(0, YS * ZS, given, 0)


def shards(gradients, projection, queries):
    rows, feats = gradients.shape
    width = projection.shape[1]
    count = queries.shape[0]
    part_rows = count // XS
    deep = feats + part_rows
    spans = {"A": halves(0, ROWS_A), "B": halves(ROWS_A, deep)}
    actions, _ = plan(ROWS_A * width * 2, (deep - ROWS_A) * width * 2)
    keys = sorted((action[1] for action in actions if action[0] == "wait"), key=lambda k: (k[0], k[3] > 0, k))
    ids = {key: k for k, key in enumerate(keys)}
    dma = pltpu.SemaphoreType.DMA
    return pl.pallas_call(
        functools.partial(kernel, actions, spans, ids),
        out_shape=jax.ShapeDtypeStruct((rows // XS, count), jnp.float32),
        in_specs=[pl.BlockSpec(memory_space=pl.ANY)] * 3,
        out_specs=pl.BlockSpec(memory_space=pltpu.VMEM),
        scratch_shapes=[
            pltpu.VMEM((XS, rows, feats), jnp.bfloat16),
            pltpu.VMEM((feats, width), jnp.bfloat16),
            pltpu.VMEM((count, width), jnp.bfloat16),
            pltpu.VMEM((2 * YS * ZS, deep, width), jnp.bfloat16),
            pltpu.VMEM((ZS // 2, rows, YS * width), jnp.float32),
            pltpu.VMEM((XS, rows // XS + 16, count), jnp.float32),
            pltpu.VMEM((XS - 1, rows // XS + 16, count), jnp.float32),
            dma((5,)), dma((4,)), dma((4,)), dma((2,)), dma((2,)),
            dma((len(keys),)), dma((len(keys),)), dma((YS * ZS,)), dma((YS * ZS,)), dma((3,)), dma((3,)),
        ],
        compiler_params=pltpu.CompilerParams(
            collective_id=0, has_side_effects=True, vmem_limit_bytes=56 * 2**20
        ),
    )(gradients, projection, queries)


def solution(mesh):
    placed = (P("seq", "layer"), P("layer", "seq"), P(None, "seq"))
    return jax.shard_map(
        shards, mesh=mesh, in_specs=placed, out_specs=P(("seq", "layer"), None), check_vma=False
    )
```

time: 161 us -> 89.3 us (0.55)
  Pallas kernels: 0 us -> 87.7 us
  blocking collectives: 61.2 us -> 0 us
  waiting for transfers between devices: 56.9 us -> 0 us
  between operations: 13.5 us -> 0.01 us
  matrix products: 11.1 us -> 0 us
  starting transfers between devices: 10.8 us -> 0 us
  local copies, waits for them, and re-layouts: 4.64 us -> 1.47 us
  other arithmetic: 1.97 us -> 0 us
    pallas_call x0 -> x1, Pallas kernels: none -> 87.7 us  [shards(): pl.pallas_call(functools.partial(kernel, actions, spans, ids), out_shape=...]
    all_to_all x2 -> x0, blocking collectives: 61.2 us -> none  [the longest x1 51 us: copy_for_each(): lax.all_to_all(jnp.broadcast_to(array[None], (size, *array.shape)), axis,...]
    all_to_all x3 -> x0, waiting for transfers between devices: 37.6 us -> none  [the longest x2 29.9 us: copy_for_each(): lax.all_to_all(jnp.broadcast_to(array[None], (size, *array.shape)), axis,...]
    all_gather x1 -> x0, waiting for transfers between devices: 19.4 us -> none  [finish_blocks(): lax.all_gather(block, 'seq', axis=1, tiled=True)]
    dot_general x2 -> x0, matrix products: 11.1 us -> none  [the longest x1 9.43 us: finish_blocks(): jnp.dot(full_grads, lax.all_gather(block, 'seq', axis=1, tiled=True), pre...]
    all_to_all x3 -> x0, starting transfers between devices: 10.8 us -> none  [the longest x2 6.85 us: copy_for_each(): lax.all_to_all(jnp.broadcast_to(array[None], (size, *array.shape)), axis,...]
    broadcast_in_dim x3 -> x0, local copies, waits for them, and re-layouts: 2.22 us -> none  [copy_for_each(): jnp.broadcast_to(array[None], (size, *array.shape))]
  transfers between devices with their start and end apart: 4 -> 0, of which waited for: 4 -> 0; matrix products, arithmetic and copies ran while one was open for 2% -> 0% of each run, Pallas kernels for 0% -> 0%
where the time goes in v1:
time: 89.3 us; the launch traced here: 89.1 us
  Pallas kernels  87.7 us (98%)
  local copies, waits for them, and re-layouts  1.47 us (2%)
    pallas_call x1, Pallas kernels, shards(): pl.pallas_call(functools.partial(kernel, actions, spans, ids), out_shape=...  87.7 us

profile of v1, /device:TPU:1, one launch (start us, length us, event | category | flops | bytes accessed | tf_op | source)
XLA Modules:
  0.0 89.1 jit_solution(17117202380254837138)
XLA Ops:
  0.0 87.7 %shard_map.37 = f32[64,256]{1,0:T(8,128)} custom-call(bf16[256,1024]{1,0:T(8,128)(2,1)} %g_hbm.1, bf16[1024,128]{1,0:T(8,128)(2,1)} %p_hbm.1, bf16[256,128]{1,0:T(8,128)(2,1)} %q_hbm.1), custom_call_target="tpu_custom_call" | custom-call | tf_op jit(solution)/shard_map/pallas_call | solution.py:378
  87.7 1.5 %copy.5 = f32[64,256]{1,0:T(8,128)} copy(f32[64,256]{1,0:T(8,128)} %shard_map.37) | data formatting | bytes 131072

commit v2 on v1

--- a/solution.py
+++ b/solution.py
@@ -82,11 +82,21 @@
                 quads.append((now, oz, 0))
                 quads.append((now + 2.0, oz, 1))
 
-    complete(("A", 0, 0, 0))
-    complete(("B", 0, 0, 0))
+    for part in ("A", "B"):
+        actions.append(("own", part))
+        complete((part, 0, 0, 0))
+        now += 2.0
     got = {}
     gathered = False
+    early = False
     while arrivals or quads or not gathered:
+        if not early and len(mine) == ZS and all(n == YS for oz, n in mine.items() if oz != 4) and not any(
+            q[1] != 4 for q in quads
+        ):
+            for oz in (0, 2, 6):
+                actions.append(("finish", oz))
+            now += 1.2
+            early = True
         if not gathered and now >= gather_us:
             actions.append(("gradients",))
             gathered = True
@@ -112,17 +122,18 @@
         if not gathered:
             nexts.append(gather_us)
         now = max(now + 1e-6, min(nexts))
+    actions.append(("finish", 4))
     return actions, now
 
 
-def kernel(actions, spans, ids, g_hbm, p_hbm, q_hbm, out_ref, gall, pin, qin, buf, acc, fsend, frecv,
-           local, gs, gr, ts, tr, ms, mr, ds, dr, fs, fr):
+def kernel(actions, spans, ids, g_hbm, p_hbm, q_hbm, out_ref, gall, pin, qin, buf, acc, prods, rsq, qsq,
+           fsend, frecv, lines, local, gs, gr, ts, tr, ms, mr, ds, dr, fs, fr):
     s, a = lax.axis_index("seq"), lax.axis_index("layer")
     core, z, y = s % 2, (s // 2) % ZS, s // (2 * ZS)
     feats, width = p_hbm.shape
     part_rows = q_hbm.shape[0] // XS
-    mine = 2 * (z % 2) + core
-    swap_s = s - mine + a
+    mine = z % 2 + 2 * core
+    swap_s = s - 2 * (z % 2) - core + 2 * (a % 2) + a // 2
     partner = s + 1 - 2 * core
 
     def at(yy, zz):
@@ -170,22 +181,30 @@
         pl.semaphore_wait(barrier, len(around))
 
     q_rows = qin.at[pl.ds(pl.multiple_of(a * part_rows, part_rows), part_rows)]
-    p_swap = remote(pin, buf.at[swap_s, pl.ds(0, feats)], ts.at[0], tr.at[0], (swap_s, mine))
-    q_swap = remote(q_rows, buf.at[swap_s, pl.ds(feats, part_rows)], ts.at[1], tr.at[1], (swap_s, mine))
-    p_stay = pltpu.make_async_copy(pin, buf.at[s, pl.ds(0, feats)], local.at[3])
-    q_stay = pltpu.make_async_copy(q_rows, buf.at[s, pl.ds(feats, part_rows)], local.at[4])
+    cuts = [(0, ROWS_A), (ROWS_A, feats), (feats, feats + part_rows)]
+
+    def swap(k, place):
+        first, last = cuts[k]
+        view = q_rows if k == 2 else pin.at[pl.ds(first, last - first)]
+        return remote(view, buf.at[place, pl.ds(first, last - first)], ts.at[k], tr.at[k], (swap_s, mine))
+
+    def stay(k):
+        first, last = cuts[k]
+        view = q_rows if k == 2 else pin.at[pl.ds(first, last - first)]
+        return pltpu.make_async_copy(view, buf.at[s, pl.ds(first, last - first)], local.at[3 + k])
+
     p_in.wait()
     q_in.wait()
 
     @pl.when(a != mine)
     def _():
-        p_swap.start()
-        q_swap.start()
+        for k in range(3):
+            swap(k, swap_s).start()
 
     @pl.when(a == mine)
     def _():
-        p_stay.start()
-        q_stay.start()
+        for k in range(3):
+            stay(k).start()
 
     left, right, far = (a + XS - 1) % XS, (a + 1) % XS, (a + 2) % XS
     half = gall.shape[1] // 2
@@ -205,15 +224,16 @@
     g_sends[0].start()
     g_sends[1].start()
 
-    @pl.when(a != mine)
-    def _():
-        remote(pin, buf.at[s, pl.ds(0, feats)], ts.at[0], tr.at[0], (swap_s, mine)).wait_recv()
-        remote(q_rows, buf.at[s, pl.ds(feats, part_rows)], ts.at[1], tr.at[1], (swap_s, mine)).wait_recv()
-
-    @pl.when(a == mine)
-    def _():
-        p_stay.wait()
-        q_stay.wait()
+    def arrived(parts):
+        @pl.when(a != mine)
+        def _():
+            for k in parts:
+                swap(k, s).wait_recv()
+
+        @pl.when(a == mine)
+        def _():
+            for k in parts:
+                stay(k).wait()
 
     def block(key):
         part, oy, oz, which = key
@@ -231,7 +251,7 @@
         acc[oz] = jnp.zeros(acc.shape[1:], jnp.float32)
 
     def quad(zz, whose):
-        layer = 2 * (zz % 2) + whose
+        layer = zz % 2 + 2 * whose
         for pair in range(2):
             right_side = jnp.concatenate(
                 [buf[(yy * ZS + zz) * 2 + whose, pl.ds(0, feats), :] for yy in (2 * pair, 2 * pair + 1)], axis=1
@@ -239,9 +259,44 @@
             columns = pl.ds(pair * 2 * width, 2 * width)
             acc[zz // 2, :, columns] += jnp.dot(gall[layer], right_side, preferred_element_type=jnp.float32)
 
+    rows = gall.shape[1]
+    prods[...] = jnp.zeros(prods.shape, jnp.float32)
+    rsq[...] = jnp.zeros(rsq.shape, jnp.float32)
+    qsq[...] = jnp.zeros(qsq.shape, jnp.float32)
+
+    def finish(group):
+        sketch = acc[group].astype(jnp.bfloat16)
+        wide = sketch.astype(jnp.float32)
+        asked = jnp.concatenate(
+            [
+                jnp.concatenate(
+                    [
+                        buf[yy * 2 * ZS + group * 4 + 2 * (layer % 2) + layer // 2, pl.ds(feats, part_rows), :]
+                        for layer in range(XS)
+                    ],
+                    axis=0,
+                )
+                for yy in range(YS)
+            ],
+            axis=1,
+        )
+        asked_wide = asked.astype(jnp.float32)
+        row_part, query_part = rsq[...], qsq[...]
+        for yy in range(YS):
+            own = wide[:, yy * width : (yy + 1) * width]
+            row_part += own * own
+            ask = asked_wide[:, yy * width : (yy + 1) * width]
+            query_part += ask * ask
+        rsq[...], qsq[...] = row_part, query_part
+        prods[...] += lax.dot_general(
+            sketch, asked, (((1,), (1,)), ((), ())), preferred_element_type=jnp.float32
+        )
+
     used = {}
     for action in actions:
-        if action[0] == "send":
+        if action[0] == "own":
+            arrived((0,) if action[1] == "A" else (1, 2))
+        elif action[0] == "send":
             for link, new in action[2]:
                 source = (*action[1], new[3])
                 used[new] = link
@@ -258,6 +313,8 @@
             g_sends[3].start()
             g_waits[2].wait_recv()
             g_waits[3].wait_recv()
+        elif action[0] == "finish":
+            finish(zpos[action[1]] // 2)
         elif action[0] == "quad":
             oz, other = action[1:]
             if other:
@@ -267,39 +324,6 @@
             else:
                 quad(zpos[oz], core)
 
-    rows = gall.shape[1]
-    queries = q_hbm.shape[0]
-    products = jnp.zeros((rows, queries), jnp.float32)
-    row_squares = jnp.zeros((rows, width), jnp.float32)
-    query_squares = jnp.zeros((queries, width), jnp.float32)
-
-    def finish(group, carry):
-        products, row_squares, query_squares = carry
-        sketch = acc[group].astype(jnp.bfloat16)
-        wide = sketch.astype(jnp.float32)
-        asked = jnp.concatenate(
-            [
-                jnp.concatenate(
-                    [buf[yy * 2 * ZS + group * 4 + layer, pl.ds(feats, part_rows), :] for layer in range(XS)], axis=0
-                )
-                for yy in range(YS)
-            ],
-            axis=1,
-        )
-        asked_wide = asked.astype(jnp.float32)
-        for yy in range(YS):
-            own = wide[:, yy * width : (yy + 1) * width]
-            row_squares += own * own
-            ask = asked_wide[:, yy * width : (yy + 1) * width]
-            query_squares += ask * ask
-        products += lax.dot_general(
-            sketch, asked, (((1,), (1,)), ((), ())), preferred_element_type=jnp.float32
-        )
-        return products, row_squares, query_squares
-
-    products, row_squares, query_squares = lax.fori_loop(
-        0, acc.shape[0], finish, (products, row_squares, query_squares)
-    )
     ones = jnp.ones((8, width), jnp.float32)
 
     def along(squares):
@@ -309,30 +333,32 @@
         )
 
     block_rows = rows // XS
-    row_line, query_line = along(row_squares), along(query_squares)
+    lines[0, pl.ds(0, 8)] = along(rsq[...])
+    lines[0, pl.ds(8, 8)] = along(qsq[...])
     for target in range(XS):
-        fsend[target, pl.ds(0, block_rows)] = products[target * block_rows : (target + 1) * block_rows]
-        fsend[target, pl.ds(block_rows, 8)] = row_line
-        fsend[target, pl.ds(block_rows + 8, 8)] = query_line
+        fsend[target] = prods[target * block_rows : (target + 1) * block_rows].astype(jnp.bfloat16)
     finals = []
-    for k, link in ((1, "x+"), (3, "x-"), (2, "x2")):
+    for k, link in ((2, "x2"), (1, "x+"), (3, "x-")):
         target = (a + k) % XS
         finals.append(remote(fsend.at[target], frecv.at[k - 1], fs.at[k - 1], fr.at[k - 1], ahead[link]))
+        finals.append(remote(lines.at[0], lines.at[k], fs.at[k + 2], fr.at[k + 2], ahead[link]))
     for copy in finals:
         copy.start()
-    total = fsend[a]
+    total = prods[pl.ds(pl.multiple_of(a * block_rows, block_rows), block_rows)]
     for copy in finals:
         copy.wait_recv()
-    total = total + frecv[0] + frecv[1] + frecv[2]
+    for k in range(XS - 1):
+        total = total + frecv[k].astype(jnp.float32)
+    line = lines[0] + lines[1] + lines[2] + lines[3]
     at_row = lax.broadcasted_iota(jnp.int32, (block_rows, rows), 0) + a * block_rows
     chosen = (lax.broadcasted_iota(jnp.int32, (block_rows, rows), 1) == at_row).astype(jnp.float32)
     own_rows = lax.dot_general(
-        chosen, total[block_rows : block_rows + 8], (((1,), (1,)), ((), ())), precision=lax.Precision.HIGHEST,
+        chosen, line[0:8], (((1,), (1,)), ((), ())), precision=lax.Precision.HIGHEST,
         preferred_element_type=jnp.float32,
     )[:, 0:1]
-    asked_squares = total[block_rows + 8 : block_rows + 9]
+    asked_squares = line[8:9]
     out_ref[...] = (
-        math.sqrt(K) * total[:block_rows] * lax.rsqrt(own_rows + EPS) * lax.rsqrt(asked_squares + EPS)
+        math.sqrt(K) * total * lax.rsqrt(own_rows + EPS) * lax.rsqrt(asked_squares + EPS)
     )
 
     for copy in finals:
@@ -342,8 +368,8 @@
 
     @pl.when(a != mine)
     def _():
-        p_swap.wait_send()
-        q_swap.wait_send()
+        for k in range(3):
+            swap(k, swap_s).wait_send()
 
     groups = {}
     for key in ids:
@@ -386,10 +412,14 @@
             pltpu.VMEM((count, width), jnp.bfloat16),
             pltpu.VMEM((2 * YS * ZS, deep, width), jnp.bfloat16),
             pltpu.VMEM((ZS // 2, rows, YS * width), jnp.float32),
-            pltpu.VMEM((XS, rows // XS + 16, count), jnp.float32),
-            pltpu.VMEM((XS - 1, rows // XS + 16, count), jnp.float32),
-            dma((5,)), dma((4,)), dma((4,)), dma((2,)), dma((2,)),
-            dma((len(keys),)), dma((len(keys),)), dma((YS * ZS,)), dma((YS * ZS,)), dma((3,)), dma((3,)),
+            pltpu.VMEM((rows, count), jnp.float32),
+            pltpu.VMEM((rows, width), jnp.float32),
+            pltpu.VMEM((count, width), jnp.float32),
+            pltpu.VMEM((XS, rows // XS, count), jnp.bfloat16),
+            pltpu.VMEM((XS - 1, rows // XS, count), jnp.bfloat16),
+            pltpu.VMEM((XS, 16, count), jnp.float32),
+            dma((6,)), dma((4,)), dma((4,)), dma((3,)), dma((3,)),
+            dma((len(keys),)), dma((len(keys),)), dma((YS * ZS,)), dma((YS * ZS,)), dma((6,)), dma((6,)),
         ],
         compiler_params=pltpu.CompilerParams(
             collective_id=0, has_side_effects=True, vmem_limit_bytes=56 * 2**20

time: 89.3 us -> 84.9 us (0.951)
  Pallas kernels: 87.7 us -> 83.3 us
    pallas_call x1, Pallas kernels: 87.7 us -> 83.3 us  [shards(): pl.pallas_call(functools.partial(kernel, actions, spans, ids), out_shape=...]
where the time goes in v2:
time: 84.9 us; the launch traced here: 84.8 us
  Pallas kernels  83.3 us (98%)
  local copies, waits for them, and re-layouts  1.47 us (2%)
    pallas_call x1, Pallas kernels, shards(): pl.pallas_call(functools.partial(kernel, actions, spans, ids), out_shape=...  83.3 us

profile of v2, /device:TPU:1, one launch (start us, length us, event | category | flops | bytes accessed | tf_op | source)
XLA Modules:
  0.0 84.8 jit_solution(18149327914745895481)
XLA Ops:
  0.0 83.3 %shard_map.37 = f32[64,256]{1,0:T(8,128)} custom-call(bf16[256,1024]{1,0:T(8,128)(2,1)} %g_hbm.1, bf16[1024,128]{1,0:T(8,128)(2,1)} %p_hbm.1, bf16[256,128]{1,0:T(8,128)(2,1)} %q_hbm.1), custom_call_target="tpu_custom_call" | custom-call | tf_op jit(solution)/shard_map/pallas_call | solution.py:404
  83.3 1.5 %copy.5 = f32[64,256]{1,0:T(8,128)} copy(f32[64,256]{1,0:T(8,128)} %shard_map.37) | data formatting | bytes 131072

commit v3 on v2

--- a/solution.py
+++ b/solution.py
@@ -13,16 +13,16 @@
 K = 8192
 EPS = 1e-06
 YS, ZS, XS = 4, 8, 4
-ROWS_A = 448
-
-
-def halves(first, last):
-    mid = (first + last) // 2
-    return {0: (first, last), 1: (first, mid), 2: (mid, last)}
-
-
-def step(pos, by, size):
-    return (pos + by) % size
+PARTS = (("B", 352), ("B", 320), ("A", 416))
+
+
+def spans_of(parts):
+    spans, first = [], 0
+    for _, rows in parts:
+        mid, last = first + rows // 2, first + rows
+        spans.append({0: (first, last), 1: (first, mid), 2: (mid, last)})
+        first = last
+    return spans
 
 
 def forwards(key):
@@ -39,7 +39,7 @@
         2: [("z-", (part, oy, 3, 0))],
         3: [("z-", (part, oy, 4, 2))],
     }
-    if part == "A":
+    if PARTS[part][0] == "A":
         if oz == 0:
             out += ys if oy == 0 else on_y.get(oy, [])
             out += zs
@@ -54,13 +54,13 @@
     return out
 
 
-def plan(bytes_a, bytes_b):
-    rate, lag, quad_us, gather_us = 44e3, 1.8, 0.45, 20.0
+def plan(row_bytes):
+    rate, lag, unit_us, event_us = 46.6e3, 1.9, 0.08, 0.08
+    gathers = [20.0, 30.0]
     free = dict.fromkeys(["y+", "y-", "z+", "z-"], 0.0)
-    size = {"A": bytes_a, "B": bytes_b}
     arrivals, order, actions = [], 0, []
-    seen, whole, mine, theirs = set(), set(), {}, {}
-    quads = []
+    seen, mine, got = set(), {}, {}
+    units = []
     now = 0.0
 
     def complete(key):
@@ -69,58 +69,64 @@
         sent = []
         for link, new in forwards(key):
             start = max(now, free[link])
-            free[link] = start + size[part] / (2 if new[3] else 1) / rate
+            free[link] = start + PARTS[part][1] * row_bytes / (2 if new[3] else 1) / rate
             heapq.heappush(arrivals, (free[link] + lag, order, new))
             order += 1
             sent.append((link, new))
         actions.append(("send", key[:3], sent))
         seen.add(key[:3])
-        if ("A", oy, oz) in seen and ("B", oy, oz) in seen:
+        if all((p, oy, oz) in seen for p in range(len(PARTS))):
             actions.append(("share", oy, oz))
             mine[oz] = mine.get(oz, 0) + 1
             if mine[oz] == YS:
-                quads.append((now, oz, 0))
-                quads.append((now + 2.0, oz, 1))
-
-    for part in ("A", "B"):
-        actions.append(("own", part))
-        complete((part, 0, 0, 0))
-        now += 2.0
-    got = {}
-    gathered = False
-    early = False
-    while arrivals or quads or not gathered:
-        if not early and len(mine) == ZS and all(n == YS for oz, n in mine.items() if oz != 4) and not any(
-            q[1] != 4 for q in quads
+                units.extend((now, oz, 0, k) for k in range(4))
+                units.extend((now + 2.0, oz, 1, k) for k in range(4))
+
+    at = 4.0
+    for part, (_, rows) in enumerate(PARTS):
+        at += rows * row_bytes / rate
+        heapq.heappush(arrivals, (at, order, (part, 0, 0, 0)))
+        order += 1
+    gathered, early = 0, False
+
+    def compute():
+        nonlocal now
+        ready = sorted(u for u in units if u[0] <= now)
+        if gathered < 2 or not ready:
+            return False
+        units.remove(ready[0])
+        actions.append(("unit", *ready[0][1:]))
+        now += unit_us
+        return True
+
+    while arrivals or units or gathered < 2:
+        if gathered < 2 and now >= gathers[gathered]:
+            actions.append(("gradients", gathered))
+            gathered += 1
+        if not early and sum(mine.get(oz, 0) for oz in range(ZS) if oz != 4) == YS * (ZS - 1) and all(
+            u[1] == 4 for u in units
         ):
             for oz in (0, 2, 6):
                 actions.append(("finish", oz))
-            now += 1.2
+                now += 0.1
             early = True
-        if not gathered and now >= gather_us:
-            actions.append(("gradients",))
-            gathered = True
         if arrivals and arrivals[0][0] <= now:
             _, _, key = heapq.heappop(arrivals)
-            actions.append(("wait", key))
-            now += 0.08
-            part, oy, oz, half = key
-            if half:
+            actions.append(("wait", key) if any(key[1:3]) else ("own", key[0]))
+            now += event_us
+            if key[3]:
                 got[key[:3]] = got.get(key[:3], 0) + 1
                 if got[key[:3]] == 2:
                     complete(key)
             else:
                 complete(key)
+            compute()
             continue
-        ready = sorted(q for q in quads if q[0] <= now)
-        if gathered and ready:
-            quads.remove(ready[0])
-            actions.append(("quad", ready[0][1], ready[0][2]))
-            now += quad_us
+        if (not arrivals or arrivals[0][0] > now + 1.5 * unit_us) and compute():
             continue
-        nexts = [a[0] for a in arrivals[:1]] + ([min(quads)[0]] if quads and gathered else [])
-        if not gathered:
-            nexts.append(gather_us)
+        nexts = [a[0] for a in arrivals[:1]] + ([min(units)[0]] if units and gathered == 2 else [])
+        if gathered < 2:
+            nexts.append(gathers[gathered])
         now = max(now + 1e-6, min(nexts))
     actions.append(("finish", 4))
     return actions, now
@@ -181,16 +187,18 @@
         pl.semaphore_wait(barrier, len(around))
 
     q_rows = qin.at[pl.ds(pl.multiple_of(a * part_rows, part_rows), part_rows)]
-    cuts = [(0, ROWS_A), (ROWS_A, feats), (feats, feats + part_rows)]
+    cuts = [span[0] for span in spans]
+    last_part = len(cuts) - 1
+    cuts = [*cuts[:-1], (cuts[-1][0], feats), (feats, feats + part_rows)]
 
     def swap(k, place):
         first, last = cuts[k]
-        view = q_rows if k == 2 else pin.at[pl.ds(first, last - first)]
+        view = q_rows if k > last_part else pin.at[pl.ds(first, last - first)]
         return remote(view, buf.at[place, pl.ds(first, last - first)], ts.at[k], tr.at[k], (swap_s, mine))
 
     def stay(k):
         first, last = cuts[k]
-        view = q_rows if k == 2 else pin.at[pl.ds(first, last - first)]
+        view = q_rows if k > last_part else pin.at[pl.ds(first, last - first)]
         return pltpu.make_async_copy(view, buf.at[s, pl.ds(first, last - first)], local.at[3 + k])
 
     p_in.wait()
@@ -198,12 +206,12 @@
 
     @pl.when(a != mine)
     def _():
-        for k in range(3):
+        for k in range(len(cuts)):
             swap(k, swap_s).start()
 
     @pl.when(a == mine)
     def _():
-        for k in range(3):
+        for k in range(len(cuts)):
             stay(k).start()
 
     left, right, far = (a + XS - 1) % XS, (a + 1) % XS, (a + 2) % XS
@@ -250,14 +258,14 @@
     for oz in range(acc.shape[0]):
         acc[oz] = jnp.zeros(acc.shape[1:], jnp.float32)
 
-    def quad(zz, whose):
-        layer = zz % 2 + 2 * whose
-        for pair in range(2):
-            right_side = jnp.concatenate(
-                [buf[(yy * ZS + zz) * 2 + whose, pl.ds(0, feats), :] for yy in (2 * pair, 2 * pair + 1)], axis=1
-            )
-            columns = pl.ds(pair * 2 * width, 2 * width)
-            acc[zz // 2, :, columns] += jnp.dot(gall[layer], right_side, preferred_element_type=jnp.float32)
+    def unit(zz, whose, k):
+        layer, pair = zz % 2 + 2 * whose, k // 2
+        deep = pl.ds(k % 2 * (feats // 2), feats // 2)
+        right_side = jnp.concatenate(
+            [buf[(yy * ZS + zz) * 2 + whose, deep, :] for yy in (2 * pair, 2 * pair + 1)], axis=1
+        )
+        columns = pl.ds(pair * 2 * width, 2 * width)
+        acc[zz // 2, :, columns] += jnp.dot(gall[layer, :, deep], right_side, preferred_element_type=jnp.float32)
 
     rows = gall.shape[1]
     prods[...] = jnp.zeros(prods.shape, jnp.float32)
@@ -295,7 +303,7 @@
     used = {}
     for action in actions:
         if action[0] == "own":
-            arrived((0,) if action[1] == "A" else (1, 2))
+            arrived((action[1],) if action[1] < last_part else (last_part, last_part + 1))
         elif action[0] == "send":
             for link, new in action[2]:
                 source = (*action[1], new[3])
@@ -307,22 +315,18 @@
             key = action[1]
             message(used[key], key, block(key)).wait_recv()
         elif action[0] == "gradients":
-            g_waits[0].wait_recv()
-            g_sends[2].start()
-            g_waits[1].wait_recv()
-            g_sends[3].start()
-            g_waits[2].wait_recv()
-            g_waits[3].wait_recv()
+            for k in (0, 1) if action[1] == 0 else (2, 3):
+                g_waits[k].wait_recv()
+                if k < 2:
+                    g_sends[k + 2].start()
         elif action[0] == "finish":
             finish(zpos[action[1]] // 2)
-        elif action[0] == "quad":
-            oz, other = action[1:]
-            if other:
+        elif action[0] == "unit":
+            oz, other, k = action[1:]
+            if other and k == 0:
                 for oy in range(YS):
                     shared(oy, oz, 1 - core).wait_recv()
-                quad(zpos[oz], 1 - core)
-            else:
-                quad(zpos[oz], core)
+            unit(zpos[oz], 1 - core if other else core, k)
 
     ones = jnp.ones((8, width), jnp.float32)
 
@@ -368,7 +372,7 @@
 
     @pl.when(a != mine)
     def _():
-        for k in range(3):
+        for k in range(len(cuts)):
             swap(k, swap_s).wait_send()
 
     groups = {}
@@ -396,8 +400,9 @@
     count = queries.shape[0]
     part_rows = count // XS
     deep = feats + part_rows
-    spans = {"A": halves(0, ROWS_A), "B": halves(ROWS_A, deep)}
-    actions, _ = plan(ROWS_A * width * 2, (deep - ROWS_A) * width * 2)
+    assert sum(part[1] for part in PARTS) == deep
+    spans = spans_of(PARTS)
+    actions, _ = plan(width * 2)
     keys = sorted((action[1] for action in actions if action[0] == "wait"), key=lambda k: (k[0], k[3] > 0, k))
     ids = {key: k for k, key in enumerate(keys)}
     dma = pltpu.SemaphoreType.DMA
@@ -418,7 +423,7 @@
             pltpu.VMEM((XS, rows // XS, count), jnp.bfloat16),
             pltpu.VMEM((XS - 1, rows // XS, count), jnp.bfloat16),
             pltpu.VMEM((XS, 16, count), jnp.float32),
-            dma((6,)), dma((4,)), dma((4,)), dma((3,)), dma((3,)),
+            dma((4 + len(PARTS),)), dma((4,)), dma((4,)), dma((1 + len(PARTS),)), dma((1 + len(PARTS),)),
             dma((len(keys),)), dma((len(keys),)), dma((YS * ZS,)), dma((YS * ZS,)), dma((6,)), dma((6,)),
         ],
         compiler_params=pltpu.CompilerParams(

time: 84.9 us -> 79.1 us (0.932)
  Pallas kernels: 83.3 us -> 77.5 us
    pallas_call x1, Pallas kernels: 83.3 us -> 77.5 us  [shards(): pl.pallas_call(functools.partial(kernel, actions, spans, ids), out_shape=...]
where the time goes in v3:
time: 79.1 us; the launch traced here: 79 us
  Pallas kernels  77.5 us (98%)
  local copies, waits for them, and re-layouts  1.47 us (2%)
    pallas_call x1, Pallas kernels, shards(): pl.pallas_call(functools.partial(kernel, actions, spans, ids), out_shape=...  77.5 us

profile of v3, /device:TPU:1, one launch (start us, length us, event | category | flops | bytes accessed | tf_op | source)
XLA Modules:
  0.0 79.0 jit_solution(12565879104533672627)
XLA Ops:
  0.0 77.5 %shard_map.37 = f32[64,256]{1,0:T(8,128)} custom-call(bf16[256,1024]{1,0:T(8,128)(2,1)} %g_hbm.1, bf16[1024,128]{1,0:T(8,128)(2,1)} %p_hbm.1, bf16[256,128]{1,0:T(8,128)(2,1)} %q_hbm.1), custom_call_target="tpu_custom_call" | custom-call | tf_op jit(solution)/shard_map/pallas_call | solution.py:409
  77.5 1.5 %copy.5 = f32[64,256]{1,0:T(8,128)} copy(f32[64,256]{1,0:T(8,128)} %shard_map.37) | data formatting | bytes 131072

commit v4 on v3

v4 whole, which is shorter than its diff:
```python
import functools
import heapq
import math

import jax
import jax.numpy as jnp
from jax import lax
from jax.experimental import pallas as pl
from jax.experimental.pallas import tpu as pltpu
from jax.sharding import PartitionSpec as P

MESH = pl.DeviceIdType.MESH
K = 8192
EPS = 1e-06
XS, YS, ZS = 4, 4, 8
RING = ZS // 2
PARTS = (("B", 480), ("B", 480), ("A", 128))


def spans_of(parts):
    spans, first = [], 0
    for _, rows in parts:
        mid, last = first + rows // 2, first + rows
        spans.append({0: (first, last), 1: (first, mid), 2: (mid, last)})
        first = last
    return spans


def forwards(key):
    part, oy, oz, half = key
    own_y = [("y+", (part, 3, oz, 0)), ("y-", (part, 1, oz, 0))]
    own_z = [("z+", (part, oy, 3, 0)), ("z-", (part, oy, 1, 0))]
    on_y = {0: own_y, 3: [("y+", (part, 2, oz, 1))], 1: [("y-", (part, 2, oz, 2))], 2: []}
    on_z = {0: own_z, 3: [("z+", (part, oy, 2, 1))], 1: [("z-", (part, oy, 2, 2))], 2: []}
    if PARTS[part][0] == "A":
        return on_y[oy] + own_z if oz == 0 else on_z[oz]
    return on_z[oz] + own_y if oy == 0 else on_y[oy]


def plan(row_bytes, piece_bytes):
    lag, unit_us, event_us, start_us = 1.9, 0.08, 0.08, 4.0
    rate = {"y+": 46.6e3, "y-": 46.6e3, "z+": 23.3e3, "z-": 23.3e3, "x+": 46.6e3, "x-": 46.6e3}
    free = dict.fromkeys(rate, 0.0)
    free["x+"] = free["x-"] = 6.0
    arrivals, order, actions = [], 0, []
    seen, mine, got, pieces = set(), {}, {}, {0: 0, 1: 0}
    units = []
    now = 0.0

    def send(link, key, size):
        nonlocal order
        begin = max(now, free[link])
        free[link] = begin + size / rate[link]
        heapq.heappush(arrivals, (free[link] + lag, order, key))
        order += 1

    def at_time(when, key):
        nonlocal order
        heapq.heappush(arrivals, (when, order, key))
        order += 1

    def complete(key):
        part, oy, oz, half = key
        sent = forwards(key)
        for link, new in sent:
            send(link, new, PARTS[part][1] * row_bytes / (2 if new[3] else 1))
        actions.append(("send", key[:3], sent))
        seen.add(key[:3])
        if all((p, oy, oz) in seen for p in range(len(PARTS))):
            actions.append(("share", oy, oz))
            whole = (oy % 2, oz)
            mine[whole] = mine.get(whole, 0) + 1
            if mine[whole] == 2:
                for group in range(2):
                    units.extend((now, oy % 2, oz, 0, group, k) for k in range(2))
                    units.extend((now + 2.0, oy % 2, oz, 1, group, k) for k in range(2))

    def offer(group, h):
        send("x+", ("G", group, 3, h), piece_bytes)
        send("x-", ("G", group, 1, h), piece_bytes)

    at = start_us
    for part, (_, rows) in enumerate(PARTS):
        at += rows * row_bytes / 46.6e3
        at_time(at, (part, 0, 0, 0))
    offer(0, 0)
    offer(0, 1)
    at_time(10.0, ("W", 0))
    at_time(20.0, ("W", 1))
    done = {(oz, group): 0 for oz in range(RING) for group in range(2)}

    def compute():
        nonlocal now
        ready = sorted(u for u in units if u[0] <= now and pieces[u[4]] == 6)
        if not ready:
            return False
        pick = ready[0]
        units.remove(pick)
        actions.append(("unit", *pick[1:]))
        now += unit_us
        done[pick[2], pick[4]] += 1
        if done[pick[2], pick[4]] == 8:
            actions.append(("finish", pick[2], pick[4]))
            now += unit_us
        return True

    while arrivals or units:
        if arrivals and arrivals[0][0] <= now:
            _, _, key = heapq.heappop(arrivals)
            now += event_us
            if key[0] == "W":
                actions.append(("swapped", key[1]))
                offer(1, key[1])
            elif key[0] == "G":
                actions.append(("gradients", *key[1:]))
                pieces[key[1]] += 1
                if key[2:] == (3, 0):
                    send("x+", ("G", key[1], 2, 0), piece_bytes)
                elif key[2:] == (1, 1):
                    send("x-", ("G", key[1], 2, 1), piece_bytes)
            else:
                actions.append(("wait", key) if any(key[1:3]) else ("own", key[0]))
                if key[3]:
                    got[key[:3]] = got.get(key[:3], 0) + 1
                    if got[key[:3]] == 2:
                        complete(key)
                else:
                    complete(key)
            compute()
            continue
        if (not arrivals or arrivals[0][0] > now + 1.5 * unit_us) and compute():
            continue
        nexts = [a[0] for a in arrivals[:1]] + [u[0] for u in units if pieces[u[4]] == 6]
        now = max(now + 1e-6, min(nexts))
    return actions, now


def kernel(actions, spans, ids, g_hbm, p_hbm, q_hbm, out_ref, gall, pin, qin, buf, acc, prods, rsq, qsq,
           fsend, frecv, lsend, lrecv, local, ws, wr, gs, gr, ts, tr, ms, mr, ds, dr, fs, fr):
    s, a = lax.axis_index("seq"), lax.axis_index("layer")
    core, z, y = s % 2, (s // 2) % ZS, s // (2 * ZS)
    feats, width = p_hbm.shape
    rows, queries = g_hbm.shape[0], q_hbm.shape[0]
    part_rows = queries // XS
    mine = y % 2 + 2 * core
    group = z % 2
    partner = s + 1 - 2 * core

    def seq(yy, zz, cc):
        return (yy * ZS + zz) * 2 + cc

    def slot(yy, jj, cc):
        return (yy * RING + jj) * 2 + cc

    swap_y, swap_core = y - y % 2 + a % 2, a // 2
    swap_to = (seq(swap_y, z, swap_core), mine)
    across = z + 1 - 2 * group
    ahead = {
        "y+": (seq((y + 1) % YS, z, core), a),
        "y-": (seq((y + YS - 1) % YS, z, core), a),
        "z+": (seq(y, (z + 2) % ZS, core), a),
        "z-": (seq(y, (z + ZS - 2) % ZS, core), a),
        "x+": (s, (a + 1) % XS),
        "x-": (s, (a + XS - 1) % XS),
    }
    targets = [(3 + k, 1, (a + k) % XS, (seq(y, across, core), (a + k) % XS)) for k in (2, 1, 3, 0)]
    targets += [(k - 1, 0, (a + k) % XS, (s, (a + k) % XS)) for k in (2, 1, 3)]
    ypos = [(y + k) % YS for k in range(YS)]
    jpos = [(z // 2 + k) % RING for k in range(RING)]

    def remote(src, dst, send, recv, to):
        return pltpu.make_async_remote_copy(
            src_ref=src, dst_ref=dst, send_sem=send, recv_sem=recv, device_id=to, device_id_type=MESH
        )

    p_in = pltpu.make_async_copy(p_hbm, pin, local.at[0])
    q_in = pltpu.make_async_copy(q_hbm, qin, local.at[1])
    g_in = pltpu.make_async_copy(g_hbm, gall.at[group, a], local.at[2])
    p_in.start()
    q_in.start()
    g_in.start()

    barrier = pltpu.get_barrier_semaphore()
    around = [*ahead.values(), *(target[3] for target in targets), (partner, a)]
    del around[4:6]
    for device in around:
        pl.semaphore_signal(barrier, inc=1, device_id=device, device_id_type=MESH)

    @pl.when(a != mine)
    def _():
        pl.semaphore_signal(barrier, inc=1, device_id=swap_to, device_id_type=MESH)
        pl.semaphore_wait(barrier, len(around) + 1)

    @pl.when(a == mine)
    def _():
        pl.semaphore_wait(barrier, len(around))

    q_rows = qin.at[pl.ds(pl.multiple_of(a * part_rows, part_rows), part_rows)]
    cuts = [span[0] for span in spans]
    last_part = len(cuts) - 1
    cuts = [*cuts[:-1], (cuts[-1][0], feats), (feats, feats + part_rows)]
    here = slot(y, z // 2, core)

    def swap(k, place):
        first, last = cuts[k]
        view = q_rows if k > last_part else pin.at[pl.ds(first, last - first)]
        return remote(view, buf.at[place, pl.ds(first, last - first)], ts.at[k], tr.at[k], swap_to)

    def stay(k):
        first, last = cuts[k]
        view = q_rows if k > last_part else pin.at[pl.ds(first, last - first)]
        return pltpu.make_async_copy(view, buf.at[here, pl.ds(first, last - first)], local.at[3 + k])

    p_in.wait()
    q_in.wait()

    @pl.when(a != mine)
    def _():
        for k in range(len(cuts)):
            swap(k, slot(swap_y, z // 2, swap_core)).start()

    @pl.when(a == mine)
    def _():
        for k in range(len(cuts)):
            stay(k).start()

    def arrived(parts):
        @pl.when(a != mine)
        def _():
            for k in parts:
                swap(k, here).wait_recv()

        @pl.when(a == mine)
        def _():
            for k in parts:
                stay(k).wait()

    piece = rows // 2

    def handed(h, whose):
        view = gall.at[whose, a, pl.ds(h * piece, piece)]
        return remote(view, view, ws.at[h], wr.at[h], (seq(y, across, core), a))

    def ringed(other, came, h, layer):
        view = gall.at[1 - group if other else group, layer, pl.ds(h * piece, piece)]
        k = other * 6 + {3: 0, 1: 2, 2: 4}[came] + h
        link = {3: "x+", 1: "x-", 2: "x-" if h else "x+"}[came]
        return remote(view, view, gs.at[k], gr.at[k], ahead[link])

    left, right, far = (a + XS - 1) % XS, (a + 1) % XS, (a + 2) % XS
    g_in.wait()
    handed(0, group).start()
    for h in range(2):
        ringed(0, 3, h, a).start()
        ringed(0, 1, h, a).start()

    def block(key):
        part, oy, oz, which = key
        first, last = spans[part][which]
        return buf.at[slot(ypos[oy], jpos[oz], core), pl.ds(first, last - first)]

    def message(link, key, view):
        return remote(view, view, ms.at[ids[key]], mr.at[ids[key]], ahead[link])

    def shared(oy, oz, whose):
        view = buf.at[slot(ypos[oy], jpos[oz], whose)]
        return remote(view, view, ds.at[oy * RING + oz], dr.at[oy * RING + oz], (partner, a))

    for ref in (acc, prods, rsq, qsq):
        ref[...] = jnp.zeros(ref.shape, jnp.float32)

    def unit(parity, jj, whose, rowset, k):
        layer = parity + 2 * whose
        deep = pl.ds(k * (feats // 2), feats // 2)
        right_side = jnp.concatenate([buf[slot(parity + yy, jj, whose), deep, :] for yy in (0, 2)], axis=1)
        acc[jj, rowset] += jnp.dot(gall[rowset, layer, :, deep], right_side, preferred_element_type=jnp.float32)

    def finish(jj, rowset, other):
        sketch = acc[jj, rowset].astype(jnp.bfloat16)
        wide = sketch.astype(jnp.float32)
        asked = jnp.concatenate(
            [
                jnp.concatenate(
                    [buf[slot(layer % 2 + yy, jj, layer // 2), pl.ds(feats, part_rows), :] for layer in range(XS)],
                    axis=0,
                )
                for yy in (0, 2)
            ],
            axis=1,
        )
        own = wide * wide
        rsq[other] += own[:, :width] + own[:, width:]
        if not other:
            asked_wide = asked.astype(jnp.float32)
            ask = asked_wide * asked_wide
            qsq[...] += ask[:, :width] + ask[:, width:]
        prods[other] += lax.dot_general(
            sketch, asked, (((1,), (1,)), ((), ())), preferred_element_type=jnp.float32
        )

    used = {}
    for action in actions:
        if action[0] == "own":
            arrived((action[1],) if action[1] < last_part else (last_part, last_part + 1))
        elif action[0] == "send":
            for link, new in action[2]:
                used[new] = link
                message(link, new, block((*action[1], new[3]))).start()
            if action[1] == (0, 0, 0):
                handed(1, group).start()
        elif action[0] == "share":
            shared(action[1], action[2], core).start()
        elif action[0] == "wait":
            key = action[1]
            message(used[key], key, block(key)).wait_recv()
        elif action[0] == "swapped":
            h = action[1]
            handed(h, 1 - group).wait_recv()
            ringed(1, 3, h, a).start()
            ringed(1, 1, h, a).start()
        elif action[0] == "gradients":
            other, came, h = action[1:]
            ringed(other, came, h, {3: left, 1: right, 2: far}[came]).wait_recv()
            if (came, h) == (3, 0):
                ringed(other, 2, 0, left).start()
            elif (came, h) == (1, 1):
                ringed(other, 2, 1, right).start()
        elif action[0] == "unit":
            op, oz, their, other, k = action[1:]
            if their and not other and k == 0:
                for oy in (op, op + 2):
                    shared(oy, oz, 1 - core).wait_recv()
            unit((y + op) % 2, jpos[oz], 1 - core if their else core, 1 - group if other else group, k)
        elif action[0] == "finish":
            oz, other = action[1:]
            finish(jpos[oz], 1 - group if other else group, other)

    ones = jnp.ones((8, width), jnp.float32)

    def along(squares):
        return lax.dot_general(
            ones, squares, (((1,), (1,)), ((), ())), precision=lax.Precision.HIGHEST,
            preferred_element_type=jnp.float32,
        )

    block_rows = rows // XS
    query_line = along(qsq[...])
    for other in range(2):
        lsend[other, pl.ds(0, 8)] = along(rsq[other])
        lsend[other, pl.ds(8, 8)] = query_line
        for layer in range(XS):
            fsend[other, layer] = prods[other, layer * block_rows : (layer + 1) * block_rows].astype(jnp.bfloat16)
    finals = []
    for k, other, layer, device in targets:
        finals.append(remote(fsend.at[other, layer], frecv.at[k], fs.at[k], fr.at[k], device))
        finals.append(remote(lsend.at[other], lrecv.at[k], fs.at[7 + k], fr.at[7 + k], device))
    for copy in finals:
        copy.start()
    total = prods[0, pl.ds(pl.multiple_of(a * block_rows, block_rows), block_rows)]
    line = lsend[0]
    for copy in finals:
        copy.wait_recv()
    for k in range(7):
        total = total + frecv[k].astype(jnp.float32)
        line = line + lrecv[k]
    at_row = lax.broadcasted_iota(jnp.int32, (block_rows, rows), 0) + a * block_rows
    chosen = (lax.broadcasted_iota(jnp.int32, (block_rows, rows), 1) == at_row).astype(jnp.float32)
    own_rows = lax.dot_general(
        chosen, line[0:8], (((1,), (1,)), ((), ())), precision=lax.Precision.HIGHEST,
        preferred_element_type=jnp.float32,
    )[:, 0:1]
    out_ref[...] = math.sqrt(K) * total * lax.rsqrt(own_rows + EPS) * lax.rsqrt(line[8:9] + EPS)

    for copy in finals:
        copy.wait_send()
    for h in range(2):
        handed(h, group).wait_send()

    def rung(k, carry):
        view = gall.at[0, 0, pl.ds(0, piece)]
        remote(view, view, gs.at[k], gr.at[k], (partner, a)).wait_send()
        return carry

    lax.fori_loop(0, 12, rung, 0)

    @pl.when(a != mine)
    def _():
        for k in range(len(cuts)):
            swap(k, slot(swap_y, z // 2, swap_core)).wait_send()

    groups = {}
    for key in ids:
        groups.setdefault((key[0], bool(key[3])), []).append(key)
    for keys in groups.values():
        first, view = ids[keys[0]], block(keys[0])

        def sent(k, carry, view=view):
            remote(view, view, ms.at[k], mr.at[k], (partner, a)).wait_send()
            return carry

        lax.fori_loop(first, first + len(keys), sent, 0)

    def given(k, carry):
        remote(buf.at[0], buf.at[0], ds.at[k], dr.at[k], (partner, a)).wait_send()
        return carry

    lax.fori_loop(0, YS * RING, given, 0)


def shards(gradients, projection, queries):
    rows, feats = gradients.shape
    width = projection.shape[1]
    count = queries.shape[0]
    deep = feats + count // XS
    assert sum(part[1] for part in PARTS) == deep
    spans = spans_of(PARTS)
    actions, _ = plan(width * 2, rows * feats)
    keys = sorted((action[1] for action in actions if action[0] == "wait"), key=lambda k: (k[0], k[3] > 0, k))
    ids = {key: k for k, key in enumerate(keys)}
    dma = pltpu.SemaphoreType.DMA
    cuts = len(PARTS) + 1
    return pl.pallas_call(
        functools.partial(kernel, actions, spans, ids),
        out_shape=jax.ShapeDtypeStruct((rows // XS, count), jnp.float32),
        in_specs=[pl.BlockSpec(memory_space=pl.ANY)] * 3,
        out_specs=pl.BlockSpec(memory_space=pltpu.VMEM),
        scratch_shapes=[
            pltpu.VMEM((2, XS, rows, feats), jnp.bfloat16),
            pltpu.VMEM((feats, width), jnp.bfloat16),
            pltpu.VMEM((count, width), jnp.bfloat16),
            pltpu.VMEM((2 * YS * RING, deep, width), jnp.bfloat16),
            pltpu.VMEM((RING, 2, rows, 2 * width), jnp.float32),
            pltpu.VMEM((2, rows, count), jnp.float32),
            pltpu.VMEM((2, rows, width), jnp.float32),
            pltpu.VMEM((count, width), jnp.float32),
            pltpu.VMEM((2, XS, rows // XS, count), jnp.bfloat16),
            pltpu.VMEM((7, rows // XS, count), jnp.bfloat16),
            pltpu.VMEM((2, 16, count), jnp.float32),
            pltpu.VMEM((7, 16, count), jnp.float32),
            dma((3 + cuts,)), dma((2,)), dma((2,)), dma((12,)), dma((12,)), dma((cuts,)), dma((cuts,)),
            dma((len(keys),)), dma((len(keys),)), dma((YS * RING,)), dma((YS * RING,)), dma((14,)), dma((14,)),
        ],
        compiler_params=pltpu.CompilerParams(
            collective_id=0, has_side_effects=True, vmem_limit_bytes=56 * 2**20
        ),
    )(gradients, projection, queries)


def solution(mesh):
    placed = (P("seq", "layer"), P("layer", "seq"), P(None, "seq"))
    return jax.shard_map(
        shards, mesh=mesh, in_specs=placed, out_specs=P(("seq", "layer"), None), check_vma=False
    )
```

time: 79.1 us -> 74.8 us (0.946)
  Pallas kernels: 77.5 us -> 73.2 us
    pallas_call x1, Pallas kernels: 77.5 us -> 73.2 us  [shards(): pl.pallas_call(functools.partial(kernel, actions, spans, ids), out_shape=...]
where the time goes in v4:
time: 74.8 us; the launch traced here: 74.7 us
  Pallas kernels  73.2 us (98%)
  local copies, waits for them, and re-layouts  1.47 us (2%)
    pallas_call x1, Pallas kernels, shards(): pl.pallas_call(functools.partial(kernel, actions, spans, ids), out_shape=...  73.2 us

profile of v4, /device:TPU:1, one launch (start us, length us, event | category | flops | bytes accessed | tf_op | source)
XLA Modules:
  0.0 74.7 jit_solution(2350754077496414923)
XLA Ops:
  0.0 73.2 %shard_map.37 = f32[64,256]{1,0:T(8,128)} custom-call(bf16[256,1024]{1,0:T(8,128)(2,1)} %g_hbm.1, bf16[1024,128]{1,0:T(8,128)(2,1)} %p_hbm.1, bf16[256,128]{1,0:T(8,128)(2,1)} %q_hbm.1), custom_call_target="tpu_custom_call" | custom-call | tf_op jit(solution)/shard_map/pallas_call | solution.py:422
  73.2 1.5 %copy.5 = f32[64,256]{1,0:T(8,128)} copy(f32[64,256]{1,0:T(8,128)} %shard_map.37) | data formatting | bytes 131072

commit v5 on v4

--- a/solution.py
+++ b/solution.py
@@ -14,7 +14,7 @@
 EPS = 1e-06
 XS, YS, ZS = 4, 4, 8
 RING = ZS // 2
-PARTS = (("B", 480), ("B", 480), ("A", 128))
+PARTS = (("B", 512), ("B", 576))
 
 
 def spans_of(parts):
@@ -38,13 +38,15 @@
 
 
 def plan(row_bytes, piece_bytes):
-    lag, unit_us, event_us, start_us = 1.9, 0.08, 0.08, 4.0
+    lag, unit_us, event_us, start_us = 3.2, 0.08, 0.08, 4.0
     rate = {"y+": 46.6e3, "y-": 46.6e3, "z+": 23.3e3, "z-": 23.3e3, "x+": 46.6e3, "x-": 46.6e3}
     free = dict.fromkeys(rate, 0.0)
     free["x+"] = free["x-"] = 6.0
     arrivals, order, actions = [], 0, []
-    seen, mine, got, pieces = set(), {}, {}, {0: 0, 1: 0}
-    units = []
+    mine, got = {}, {}
+    pieces = {(group, away): 0 for group in range(2) for away in range(XS)}
+    pieces[0, 0] = 2
+    units, taken = [], set()
     now = 0.0
 
     def send(link, key, size):
@@ -65,15 +67,10 @@
         for link, new in sent:
             send(link, new, PARTS[part][1] * row_bytes / (2 if new[3] else 1))
         actions.append(("send", key[:3], sent))
-        seen.add(key[:3])
-        if all((p, oy, oz) in seen for p in range(len(PARTS))):
-            actions.append(("share", oy, oz))
-            whole = (oy % 2, oz)
-            mine[whole] = mine.get(whole, 0) + 1
-            if mine[whole] == 2:
-                for group in range(2):
-                    units.extend((now, oy % 2, oz, 0, group, k) for k in range(2))
-                    units.extend((now + 2.0, oy % 2, oz, 1, group, k) for k in range(2))
+        actions.append(("share", *key[:3]))
+        mine[part, oz] = mine.get((part, oz), 0) + 1
+        if mine[part, oz] == YS:
+            units.extend((now + 2.0, oz, group, away, part) for away in (0, 1, 3, 2) for group in range(2))
 
     def offer(group, h):
         send("x+", ("G", group, 3, h), piece_bytes)
@@ -91,16 +88,19 @@
 
     def compute():
         nonlocal now
-        ready = sorted(u for u in units if u[0] <= now and pieces[u[4]] == 6)
+        ready = [u for u in units if u[0] <= now and pieces[u[2], u[3]] == 2]
         if not ready:
             return False
         pick = ready[0]
+        if (pick[4], pick[1]) not in taken:
+            actions.append(("take", pick[4], pick[1]))
+            taken.add((pick[4], pick[1]))
         units.remove(pick)
         actions.append(("unit", *pick[1:]))
         now += unit_us
-        done[pick[2], pick[4]] += 1
-        if done[pick[2], pick[4]] == 8:
-            actions.append(("finish", pick[2], pick[4]))
+        done[pick[1:3]] += 1
+        if done[pick[1:3]] == 8:
+            actions.append(("finish", *pick[1:3]))
             now += unit_us
         return True
 
@@ -110,10 +110,11 @@
             now += event_us
             if key[0] == "W":
                 actions.append(("swapped", key[1]))
+                pieces[1, 0] += 1
                 offer(1, key[1])
             elif key[0] == "G":
                 actions.append(("gradients", *key[1:]))
-                pieces[key[1]] += 1
+                pieces[key[1:3]] += 1
                 if key[2:] == (3, 0):
                     send("x+", ("G", key[1], 2, 0), piece_bytes)
                 elif key[2:] == (1, 1):
@@ -130,7 +131,7 @@
             continue
         if (not arrivals or arrivals[0][0] > now + 1.5 * unit_us) and compute():
             continue
-        nexts = [a[0] for a in arrivals[:1]] + [u[0] for u in units if pieces[u[4]] == 6]
+        nexts = [a[0] for a in arrivals[:1]] + [u[0] for u in units if pieces[u[2], u[3]] == 2]
         now = max(now + 1e-6, min(nexts))
     return actions, now
 
@@ -262,15 +263,17 @@
     def message(link, key, view):
         return remote(view, view, ms.at[ids[key]], mr.at[ids[key]], ahead[link])
 
-    def shared(oy, oz, whose):
-        view = buf.at[slot(ypos[oy], jpos[oz], whose)]
-        return remote(view, view, ds.at[oy * RING + oz], dr.at[oy * RING + oz], (partner, a))
+    def shared(part, oy, oz, whose):
+        first, last = spans[part][0]
+        view = buf.at[slot(ypos[oy], jpos[oz], whose), pl.ds(first, last - first)]
+        k = (part * YS + oy) * RING + oz
+        return remote(view, view, ds.at[k], dr.at[k], (partner, a))
 
     for ref in (acc, prods, rsq, qsq):
         ref[...] = jnp.zeros(ref.shape, jnp.float32)
 
-    def unit(parity, jj, whose, rowset, k):
-        layer = parity + 2 * whose
+    def unit(jj, rowset, layer, k):
+        parity, whose = layer % 2, layer // 2
         deep = pl.ds(k * (feats // 2), feats // 2)
         right_side = jnp.concatenate([buf[slot(parity + yy, jj, whose), deep, :] for yy in (0, 2)], axis=1)
         acc[jj, rowset] += jnp.dot(gall[rowset, layer, :, deep], right_side, preferred_element_type=jnp.float32)
@@ -309,7 +312,7 @@
             if action[1] == (0, 0, 0):
                 handed(1, group).start()
         elif action[0] == "share":
-            shared(action[1], action[2], core).start()
+            shared(*action[1:], core).start()
         elif action[0] == "wait":
             key = action[1]
             message(used[key], key, block(key)).wait_recv()
@@ -325,12 +328,12 @@
                 ringed(other, 2, 0, left).start()
             elif (came, h) == (1, 1):
                 ringed(other, 2, 1, right).start()
+        elif action[0] == "take":
+            for oy in range(YS):
+                shared(action[1], oy, action[2], 1 - core).wait_recv()
         elif action[0] == "unit":
-            op, oz, their, other, k = action[1:]
-            if their and not other and k == 0:
-                for oy in (op, op + 2):
-                    shared(oy, oz, 1 - core).wait_recv()
-            unit((y + op) % 2, jpos[oz], 1 - core if their else core, 1 - group if other else group, k)
+            oz, other, away, k = action[1:]
+            unit(jpos[oz], 1 - group if other else group, (a + away) % XS, k)
         elif action[0] == "finish":
             oz, other = action[1:]
             finish(jpos[oz], 1 - group if other else group, other)
@@ -345,9 +348,9 @@
 
     block_rows = rows // XS
     query_line = along(qsq[...])
+    upper = lax.broadcasted_iota(jnp.int32, query_line.shape, 0) < 4
     for other in range(2):
-        lsend[other, pl.ds(0, 8)] = along(rsq[other])
-        lsend[other, pl.ds(8, 8)] = query_line
+        lsend[other] = jnp.where(upper, along(rsq[other]), query_line)
         for layer in range(XS):
             fsend[other, layer] = prods[other, layer * block_rows : (layer + 1) * block_rows].astype(jnp.bfloat16)
     finals = []
@@ -366,10 +369,10 @@
     at_row = lax.broadcasted_iota(jnp.int32, (block_rows, rows), 0) + a * block_rows
     chosen = (lax.broadcasted_iota(jnp.int32, (block_rows, rows), 1) == at_row).astype(jnp.float32)
     own_rows = lax.dot_general(
-        chosen, line[0:8], (((1,), (1,)), ((), ())), precision=lax.Precision.HIGHEST,
+        chosen, line, (((1,), (1,)), ((), ())), precision=lax.Precision.HIGHEST,
         preferred_element_type=jnp.float32,
     )[:, 0:1]
-    out_ref[...] = math.sqrt(K) * total * lax.rsqrt(own_rows + EPS) * lax.rsqrt(line[8:9] + EPS)
+    out_ref[...] = math.sqrt(K) * total * lax.rsqrt(own_rows + EPS) * lax.rsqrt(line[4:5] + EPS)
 
     for copy in finals:
         copy.wait_send()
@@ -400,11 +403,15 @@
 
         lax.fori_loop(first, first + len(keys), sent, 0)
 
-    def given(k, carry):
-        remote(buf.at[0], buf.at[0], ds.at[k], dr.at[k], (partner, a)).wait_send()
-        return carry
-
-    lax.fori_loop(0, YS * RING, given, 0)
+    for part in range(len(spans)):
+        first, last = spans[part][0]
+        view = buf.at[0, pl.ds(first, last - first)]
+
+        def given(k, carry, view=view):
+            remote(view, view, ds.at[k], dr.at[k], (partner, a)).wait_send()
+            return carry
+
+        lax.fori_loop(part * YS * RING, (part + 1) * YS * RING, given, 0)
 
 
 def shards(gradients, projection, queries):
@@ -435,10 +442,10 @@
             pltpu.VMEM((count, width), jnp.float32),
             pltpu.VMEM((2, XS, rows // XS, count), jnp.bfloat16),
             pltpu.VMEM((7, rows // XS, count), jnp.bfloat16),
-            pltpu.VMEM((2, 16, count), jnp.float32),
-            pltpu.VMEM((7, 16, count), jnp.float32),
+            pltpu.VMEM((2, 8, count), jnp.float32),
+            pltpu.VMEM((7, 8, count), jnp.float32),
             dma((3 + cuts,)), dma((2,)), dma((2,)), dma((12,)), dma((12,)), dma((cuts,)), dma((cuts,)),
-            dma((len(keys),)), dma((len(keys),)), dma((YS * RING,)), dma((YS * RING,)), dma((14,)), dma((14,)),
+            dma((len(keys),)), dma((len(keys),)), dma((len(PARTS) * YS * RING,)), dma((len(PARTS) * YS * RING,)), dma((14,)), dma((14,)),
         ],
         compiler_params=pltpu.CompilerParams(
             collective_id=0, has_side_effects=True, vmem_limit_bytes=56 * 2**20

time: 74.8 us -> 71.3 us (0.953)
  Pallas kernels: 73.2 us -> 69.7 us
    pallas_call x1, Pallas kernels: 73.2 us -> 69.7 us  [shards(): pl.pallas_call(functools.partial(kernel, actions, spans, ids), out_shape=...]
where the time goes in v5:
time: 71.3 us; the launch traced here: 71.2 us
  Pallas kernels  69.7 us (98%)
  local copies, waits for them, and re-layouts  1.47 us (2%)
    pallas_call x1, Pallas kernels, shards(): pl.pallas_call(functools.partial(kernel, actions, spans, ids), out_shape=...  69.7 us
    unnamed x1, local copies, waits for them, and re-layouts  1.47 us

profile of v5, /device:TPU:1, one launch (start us, length us, event | category | flops | bytes accessed | tf_op | source)
XLA Modules:
  0.0 71.2 jit_solution(7448104608294893420)
XLA Ops:
  0.0 69.7 %shard_map.37 = f32[64,256]{1,0:T(8,128)} custom-call(bf16[256,1024]{1,0:T(8,128)(2,1)} %g_hbm.1, bf16[1024,128]{1,0:T(8,128)(2,1)} %p_hbm.1, bf16[256,128]{1,0:T(8,128)(2,1)} %q_hbm.1), custom_call_target="tpu_custom_call" | custom-call | tf_op jit(solution)/shard_map/pallas_call | solution.py:429
  69.7 1.5 %copy.5 = f32[64,256]{1,0:T(8,128)} copy(f32[64,256]{1,0:T(8,128)} %shard_map.37) | data formatting | bytes 131072

commit v6 on v5

--- a/solution.py
+++ b/solution.py
@@ -34,12 +34,12 @@
     on_z = {0: own_z, 3: [("z+", (part, oy, 2, 1))], 1: [("z-", (part, oy, 2, 2))], 2: []}
     if PARTS[part][0] == "A":
         return on_y[oy] + own_z if oz == 0 else on_z[oz]
-    return on_z[oz] + own_y if oy == 0 else on_y[oy]
+    return (own_y + own_z if oz == 0 else on_z[oz] + own_y) if oy == 0 else on_y[oy]
 
 
 def plan(row_bytes, piece_bytes):
     lag, unit_us, event_us, start_us = 3.2, 0.08, 0.08, 4.0
-    rate = {"y+": 46.6e3, "y-": 46.6e3, "z+": 23.3e3, "z-": 23.3e3, "x+": 46.6e3, "x-": 46.6e3}
+    rate = {"y+": 42e3, "y-": 42e3, "z+": 21e3, "z-": 21e3, "x+": 46.6e3, "x-": 46.6e3}
     free = dict.fromkeys(rate, 0.0)
     free["x+"] = free["x-"] = 6.0
     arrivals, order, actions = [], 0, []
@@ -70,7 +70,7 @@
         actions.append(("share", *key[:3]))
         mine[part, oz] = mine.get((part, oz), 0) + 1
         if mine[part, oz] == YS:
-            units.extend((now + 2.0, oz, group, away, part) for away in (0, 1, 3, 2) for group in range(2))
+            units.extend((now + 2.0, oz, group, away, part) for group in (1, 0) for away in (0, 1, 3, 2))
 
     def offer(group, h):
         send("x+", ("G", group, 3, h), piece_bytes)
@@ -101,6 +101,8 @@
         done[pick[1:3]] += 1
         if done[pick[1:3]] == 8:
             actions.append(("finish", *pick[1:3]))
+            if all(done[oz, pick[2]] == 8 for oz in range(RING)):
+                actions.append(("post", pick[2]))
             now += unit_us
         return True
 
@@ -293,13 +295,39 @@
         )
         own = wide * wide
         rsq[other] += own[:, :width] + own[:, width:]
-        if not other:
+        if other:
             asked_wide = asked.astype(jnp.float32)
             ask = asked_wide * asked_wide
             qsq[...] += ask[:, :width] + ask[:, width:]
         prods[other] += lax.dot_general(
             sketch, asked, (((1,), (1,)), ((), ())), preferred_element_type=jnp.float32
         )
+
+    ones = jnp.ones((8, width), jnp.float32)
+
+    def along(squares):
+        return lax.dot_general(
+            ones, squares, (((1,), (1,)), ((), ())), precision=lax.Precision.HIGHEST,
+            preferred_element_type=jnp.float32,
+        )
+
+    block_rows = rows // XS
+    finals = []
+    query_lines = []
+
+    def post(other):
+        if not query_lines:
+            query_lines.append(along(qsq[...]))
+        query_line = query_lines[0]
+        upper = lax.broadcasted_iota(jnp.int32, query_line.shape, 0) < 4
+        for layer in range(XS):
+            fsend[other, layer] = prods[other, layer * block_rows : (layer + 1) * block_rows].astype(jnp.bfloat16)
+        lsend[other] = jnp.where(upper, along(rsq[other]), query_line)
+        for k, which, layer, device in targets:
+            if which == other:
+                for source, into, sem in ((fsend.at[other, layer], frecv.at[k], k), (lsend.at[other], lrecv.at[k], 7 + k)):
+                    finals.append(remote(source, into, fs.at[sem], fr.at[sem], device))
+                    finals[-1].start()
 
     used = {}
     for action in actions:
@@ -334,31 +362,12 @@
         elif action[0] == "unit":
             oz, other, away, k = action[1:]
             unit(jpos[oz], 1 - group if other else group, (a + away) % XS, k)
+        elif action[0] == "post":
+            post(action[1])
         elif action[0] == "finish":
             oz, other = action[1:]
             finish(jpos[oz], 1 - group if other else group, other)
 
-    ones = jnp.ones((8, width), jnp.float32)
-
-    def along(squares):
-        return lax.dot_general(
-            ones, squares, (((1,), (1,)), ((), ())), precision=lax.Precision.HIGHEST,
-            preferred_element_type=jnp.float32,
-        )
-
-    block_rows = rows // XS
-    query_line = along(qsq[...])
-    upper = lax.broadcasted_iota(jnp.int32, query_line.shape, 0) < 4
-    for other in range(2):
-        lsend[other] = jnp.where(upper, along(rsq[other]), query_line)
-        for layer in range(XS):
-            fsend[other, layer] = prods[other, layer * block_rows : (layer + 1) * block_rows].astype(jnp.bfloat16)
-    finals = []
-    for k, other, layer, device in targets:
-        finals.append(remote(fsend.at[other, layer], frecv.at[k], fs.at[k], fr.at[k], device))
-        finals.append(remote(lsend.at[other], lrecv.at[k], fs.at[7 + k], fr.at[7 + k], device))
-    for copy in finals:
-        copy.start()
     total = prods[0, pl.ds(pl.multiple_of(a * block_rows, block_rows), block_rows)]
     line = lsend[0]
     for copy in finals:
@@ -372,7 +381,7 @@
         chosen, line, (((1,), (1,)), ((), ())), precision=lax.Precision.HIGHEST,
         preferred_element_type=jnp.float32,
     )[:, 0:1]
-    out_ref[...] = math.sqrt(K) * total * lax.rsqrt(own_rows + EPS) * lax.rsqrt(line[4:5] + EPS)
+    out_ref[...] = total * lax.rsqrt(own_rows + EPS) * lax.rsqrt(line[4:5] + EPS)
 
     for copy in finals:
         copy.wait_send()
@@ -450,7 +459,7 @@
         compiler_params=pltpu.CompilerParams(
             collective_id=0, has_side_effects=True, vmem_limit_bytes=56 * 2**20
         ),
-    )(gradients, projection, queries)
+    )(gradients, projection, queries) * math.sqrt(K)
 
 
 def solution(mesh):

time: 71.3 us -> 71.1 us (level)
  other arithmetic: 0 us -> 1.48 us
  local copies, waits for them, and re-layouts: 1.47 us -> 0 us
    mul x0 -> x1, other arithmetic: none -> 1.48 us  [shards(): pl.pallas_call(functools.partial(kernel, actions, spans, ids), out_shape=...]
    unnamed x1 -> x0, local copies, waits for them, and re-layouts: 1.47 us -> none
where the time goes in v6:
time: 71.1 us; the launch traced here: 71 us
  Pallas kernels  69.5 us (98%)
  other arithmetic  1.48 us (2%)
    pallas_call x1, Pallas kernels, shards(): pl.pallas_call(functools.partial(kernel, actions, spans, ids), out_shape=...  69.5 us
    mul x1, other arithmetic, shards(): pl.pallas_call(functools.partial(kernel, actions, spans, ids), out_shape=...  1.48 us

profile of v6, /device:TPU:1, one launch (start us, length us, event | category | flops | bytes accessed | tf_op | source)
XLA Modules:
  0.0 71.0 jit_solution(2439066186044521437)
XLA Ops:
  0.0 69.5 %shard_map.37 = f32[64,256]{1,0:T(8,128)} custom-call(bf16[256,1024]{1,0:T(8,128)(2,1)} %g_hbm.1, bf16[1024,128]{1,0:T(8,128)(2,1)} %p_hbm.1, bf16[256,128]{1,0:T(8,128)(2,1)} %q_hbm.1), custom_call_target="tpu_custom_call" | custom-call | tf_op jit(solution)/shard_map/pallas_call | solution.py:438
  69.5 1.5 %broadcast_multiply_fusion = f32[64,256]{1,0:T(8,128)} fusion(f32[64,256]{1,0:T(8,128)} %shard_map.37), kind=kLoop, calls=%fused_computation | loop fusion | flops 16384 | bytes 131072 | tf_op jit(solution)/shard_map/mul | solution.py:438

commit v7 on v6

--- a/solution.py
+++ b/solution.py
@@ -319,10 +319,13 @@
         if not query_lines:
             query_lines.append(along(qsq[...]))
         query_line = query_lines[0]
-        upper = lax.broadcasted_iota(jnp.int32, query_line.shape, 0) < 4
+        row_line = along(rsq[other])
+        place = lax.broadcasted_iota(jnp.int32, (8, width), 0)
         for layer in range(XS):
             fsend[other, layer] = prods[other, layer * block_rows : (layer + 1) * block_rows].astype(jnp.bfloat16)
-        lsend[other] = jnp.where(upper, along(rsq[other]), query_line)
+        row_half = jnp.where(place < 2, row_line[:, :width], row_line[:, width:])
+        query_half = jnp.where(place < 6, query_line[:, :width], query_line[:, width:])
+        lsend[other] = jnp.where(place < 4, row_half, query_half)
         for k, which, layer, device in targets:
             if which == other:
                 for source, into, sem in ((fsend.at[other, layer], frecv.at[k], k), (lsend.at[other], lrecv.at[k], 7 + k)):
@@ -375,13 +378,17 @@
     for k in range(7):
         total = total + frecv[k].astype(jnp.float32)
         line = line + lrecv[k]
+    row_squares = jnp.concatenate(
+        [jnp.broadcast_to(line[k : k + 1], line.shape) for k in (0, 2)], axis=1
+    )
+    query_squares = jnp.concatenate([line[4:5], line[6:7]], axis=1)
     at_row = lax.broadcasted_iota(jnp.int32, (block_rows, rows), 0) + a * block_rows
     chosen = (lax.broadcasted_iota(jnp.int32, (block_rows, rows), 1) == at_row).astype(jnp.float32)
     own_rows = lax.dot_general(
-        chosen, line, (((1,), (1,)), ((), ())), precision=lax.Precision.HIGHEST,
+        chosen, row_squares, (((1,), (1,)), ((), ())), precision=lax.Precision.HIGHEST,
         preferred_element_type=jnp.float32,
     )[:, 0:1]
-    out_ref[...] = total * lax.rsqrt(own_rows + EPS) * lax.rsqrt(line[4:5] + EPS)
+    out_ref[...] = total * lax.rsqrt(own_rows + EPS) * lax.rsqrt(query_squares + EPS)
 
     for copy in finals:
         copy.wait_send()
@@ -451,8 +458,8 @@
             pltpu.VMEM((count, width), jnp.float32),
             pltpu.VMEM((2, XS, rows // XS, count), jnp.bfloat16),
             pltpu.VMEM((7, rows // XS, count), jnp.bfloat16),
-            pltpu.VMEM((2, 8, count), jnp.float32),
-            pltpu.VMEM((7, 8, count), jnp.float32),
+            pltpu.VMEM((2, 8, width), jnp.float32),
+            pltpu.VMEM((7, 8, width), jnp.float32),
             dma((3 + cuts,)), dma((2,)), dma((2,)), dma((12,)), dma((12,)), dma((cuts,)), dma((cuts,)),
             dma((len(keys),)), dma((len(keys),)), dma((len(PARTS) * YS * RING,)), dma((len(PARTS) * YS * RING,)), dma((14,)), dma((14,)),
         ],

time: 71.1 us -> 70.9 us (level)
  no operation moved by 1% of the time
where the time goes in v7:
time: 70.9 us; the launch traced here: 70.7 us
  Pallas kernels  69.3 us (98%)
  other arithmetic  1.48 us (2%)
    pallas_call x1, Pallas kernels, shards(): pl.pallas_call(functools.partial(kernel, actions, spans, ids), out_shape=...  69.3 us
    mul x1, other arithmetic, shards(): pl.pallas_call(functools.partial(kernel, actions, spans, ids), out_shape=...  1.48 us

profile of v7, /device:TPU:1, one launch (start us, length us, event | category | flops | bytes accessed | tf_op | source)
XLA Modules:
  0.0 70.7 jit_solution(771141799225881061)
XLA Ops:
  0.0 69.3 %shard_map.37 = f32[64,256]{1,0:T(8,128)} custom-call(bf16[256,1024]{1,0:T(8,128)(2,1)} %g_hbm.1, bf16[1024,128]{1,0:T(8,128)(2,1)} %p_hbm.1, bf16[256,128]{1,0:T(8,128)(2,1)} %q_hbm.1), custom_call_target="tpu_custom_call" | custom-call | tf_op jit(solution)/shard_map/pallas_call | solution.py:445
  69.3 1.5 %broadcast_multiply_fusion = f32[64,256]{1,0:T(8,128)} fusion(f32[64,256]{1,0:T(8,128)} %shard_map.37), kind=kLoop, calls=%fused_computation | loop fusion | flops 16384 | bytes 131072 | tf_op jit(solution)/shard_map/mul | solution.py:445
